TPU v7x, 32 devices: a whole 2x2x4 slice. The times are simulated.
32 devices in a mesh: row: 4 (over y, x), col: 4 (over z), head: 2 (over core).
Axes of the slice: x: 2, y: 2, z: 4, core: 2. Of those that a mesh axis runs over, the one named last changes fastest.
Arguments:
- queries: bfloat16 [256, 64, 256], P('row', 'col'), may hold values from -1000 to 1000
- level_zero: bfloat16 [256, 64, 256], P('row', 'col', 'head'), may hold values from -6 to 6
- level_one: bfloat16 [128, 32, 256], P('row', 'col', 'head'), may hold values from -6 to 6
- level_two: bfloat16 [64, 16, 256], P('row', 'col', 'head'), may hold values from -6 to 6
- level_three: bfloat16 [32, 8, 256], P('row', 'col', 'head'), may hold values from -6 to 6
- tile_lists: int32 [16, 4, 4, 8], P('row', 'col'), may hold values from 0 to 63, as said below
- samples: int32 [256, 64, 128], P('row', 'col', 'head'), may hold values from 0 to 133168895, as said below
- logit_weight: bfloat16 [256, 128], P(None, 'head'), may hold values from -1 to 1
- logit_bias: float32 [128], P('head'), may hold values from -3 to 3
- output_weight: bfloat16 [256, 256], replicated, may hold values from -0.375 to 0.375
- output_bias: float32 [256], replicated, may hold values from -3 to 3
- norm_gain: float32 [256], P('head'), may hold values from 0.5 to 1.5
- norm_shift: float32 [256], P('head'), may hold values from -3 to 3
Outputs:
- updated_queries: bfloat16 [256, 64, 256], P('row', 'col', 'head')
Inputs may be any that keep to these rules, and one draw needn't show every extreme that they name: `tile_lists`: entries are tile numbers r * 4 + c. Over all lists of the query blocks that one device holds, at one level, at most 2 entries name tiles that one device holds; at each level some device is named exactly 2 times by the lists of every device. A tile may be listed more than once. `samples`: slot is below 8; at level l, pos_row and pos_col are below (16 / 2^l - 1) * 256.
All inputs are finite; a program needn't handle non-finite values.
Results may differ from a plain program's by a relative error of at most 0.004.
Values may be sent and summed in bfloat16 or wider, within the bound.
A program may use at most 128 MiB of HBM per device.

v0:
```python
import functools

import jax
import jax.numpy as jnp
from jax import lax
from jax.experimental import pallas as pl
from jax.experimental.pallas import tpu as pltpu
from jax.sharding import PartitionSpec as P

LEVELS = 4
POINTS = 4
PACK = 16
MESH = pl.DeviceIdType.MESH


def to_blocks(source, tile_rows, tile_cols, tile_side):
    channels = source.shape[2]
    shaped = source.reshape(tile_rows, tile_side, tile_cols, tile_side, channels)
    return shaped.transpose(0, 2, 1, 3, 4).reshape(
        tile_rows * tile_cols, tile_side * tile_side, channels
    )


def hat(index, start, low, high):
    return jnp.where(index == start, low, jnp.where(index == start + 1, high, 0.0))


def prepare(head_count, b, query_ref, lw_ref, lb_ref, samples_ref, point_s, corner_s):
    queries_here = query_ref.shape[1]
    hits = LEVELS * POINTS
    logits = lax.dot_general(
        lw_ref[...], query_ref[b], (((1,), (1,)), ((), ())), preferred_element_type=jnp.float32
    ) + lb_ref[...]
    logits = logits.reshape(head_count, hits, queries_here)
    shifted = jnp.exp(logits - jnp.max(logits, axis=1, keepdims=True))
    attend = shifted / jnp.sum(shifted, axis=1, keepdims=True)
    attend = attend.reshape(head_count * hits, queries_here)
    packed = samples_ref[b].T
    pos_row = (packed >> 12) & 4095
    pos_col = packed & 4095
    frac_row = (pos_row & 255).astype(jnp.float32) * (1.0 / 256.0)
    frac_col = (pos_col & 255).astype(jnp.float32) * (1.0 / 256.0)
    point_s[b, 0] = packed >> 24
    point_s[b, 1] = pos_row >> 8
    point_s[b, 2] = pos_col >> 8
    corner_s[b, 0] = attend * (1.0 - frac_row)
    corner_s[b, 1] = attend * frac_row
    corner_s[b, 2] = 1.0 - frac_col
    corner_s[b, 3] = frac_col


def weigh(sides, spans, per_block, b, h, slab, point_s, corner_s, mask_s, weight_s):
    hits = LEVELS * POINTS
    queries_here = weight_s.shape[2]
    lane_row = lax.broadcasted_iota(jnp.int32, (PACK, queries_here), 0)
    slot_row = lax.broadcasted_iota(jnp.int32, (per_block, queries_here), 0)
    level_off = 0
    for level_num in range(LEVELS):
        side = sides[level_num]
        span = spans[level_num]
        rows = [pl.ds(h * hits + level_num * POINTS + p, 1) for p in range(POINTS)]
        for p in range(POINTS):
            mask_s[p * per_block:(p + 1) * per_block, :] = jnp.where(
                slot_row == point_s[b, 0, rows[p], :], 1.0, 0.0
            )
        cols = [
            hat(lane_row % side, point_s[b, 2, rows[p], :], corner_s[b, 2, rows[p], :],
                corner_s[b, 3, rows[p], :])
            for p in range(POINTS)
        ]
        rows_per_chunk = PACK // side

        def chunk(step, carry, rows=rows, cols=cols, side=side, span=span,
                  level_off=level_off, rows_per_chunk=rows_per_chunk):
            parts = []
            for p in range(POINTS):
                index = step * rows_per_chunk
                start = point_s[b, 1, rows[p], :]
                low = corner_s[b, 0, rows[p], :]
                high = corner_s[b, 1, rows[p], :]
                if rows_per_chunk > 1:
                    across = hat(index + lane_row // side, start, low, high)
                else:
                    across = jnp.where(
                        start == index, low, jnp.where(start == index - 1, high, 0.0)
                    )
                parts.append(cols[p] * across)
            for k in range(per_block):
                total = parts[0] * mask_s[k:k + 1, :]
                for p in range(1, POINTS):
                    total = total + parts[p] * mask_s[p * per_block + k:p * per_block + k + 1, :]
                where = pl.multiple_of(level_off + k * span + step * PACK, PACK)
                weight_s[slab, pl.ds(where, PACK), :] = total.astype(jnp.bfloat16)
            return carry

        chunks = span // PACK
        if chunks == 1:
            chunk(0, 0)
        else:
            lax.fori_loop(0, chunks, chunk, 0)
        level_off += span * per_block


def exchange_kernel(sides, spans, per_block, head_count, rows, cols, capacity, local_tiles, *refs):
    (table_ref, tiles_ref, query_ref, lw_ref, lb_ref, samples_ref, fetched_ref, weights_ref) = refs[:8]
    refs = refs[8:]
    held = refs[:cols - 1]
    (ids_v, stage, point_s, corner_s, mask_s, weight_s, id_send, id_recv, col_send, col_recv,
     row_send, row_recv, own_sem, ids_sem, weight_sem) = refs[cols - 1:]
    r = lax.axis_index("row")
    c = lax.axis_index("col")
    lanes_wide = tiles_ref.shape[1]
    barrier = pltpu.get_barrier_semaphore()
    for dc in range(1, cols):
        pl.semaphore_signal(barrier, inc=1, device_id={"col": lax.rem(c + dc, cols)}, device_id_type=MESH)
    for dr in range(1, rows):
        pl.semaphore_signal(barrier, inc=1, device_id={"row": lax.rem(r + dr, rows)}, device_id_type=MESH)
    pl.semaphore_wait(barrier, cols + rows - 2)

    id_copies = []
    for dr in range(1, rows):
        to = lax.rem(r + dr, rows)
        copy = pltpu.make_async_remote_copy(
            table_ref.at[to], ids_v.at[dr], id_send.at[dr], id_recv.at[dr],
            device_id={"row": to}, device_id_type=MESH,
        )
        copy.start()
        id_copies.append(copy)
    col_copies = []
    for dc in range(1, cols):
        copy = pltpu.make_async_remote_copy(
            tiles_ref, held[dc - 1], col_send.at[dc], col_recv.at[dc],
            device_id={"col": lax.rem(c + dc, cols)}, device_id_type=MESH,
        )
        copy.start()
        col_copies.append(copy)
    own_ids = pltpu.make_async_copy(table_ref.at[r], ids_v.at[0], ids_sem)
    own_ids.start()
    own_ids.wait()
    for copy in id_copies:
        copy.wait()

    def pick(dc):
        owner_col = lax.rem(c - dc + cols, cols)
        source = tiles_ref if dc == 0 else held[dc - 1]
        out_at = (r * cols + owner_col) * capacity
        copies = []
        for turn in range(rows):
            dr = (turn + 1) % rows
            for place in range(capacity):
                off = 0
                for level_num in range(LEVELS):
                    span = spans[level_num]
                    at = (owner_col * capacity + place) * LEVELS + level_num
                    asked = jnp.broadcast_to(ids_v[dr, pl.ds(at, 1), :], (PACK, lanes_wide))
                    shape = (span // PACK, PACK, lanes_wide)
                    total = None
                    for tile in range(local_tiles):
                        mask = jnp.where(asked == tile, 1.0, 0.0).astype(jnp.bfloat16)
                        first = local_tiles * off + tile * span
                        part = source[first:first + span, :].reshape(shape) * mask[None]
                        total = part if total is None else total + part
                    stage[dr, dc, place, off:off + span, :] = total.reshape(span, lanes_wide)
                    off += span
            target = fetched_ref.at[pl.ds(out_at, capacity)]
            if dr == 0:
                copy = pltpu.make_async_copy(stage.at[dr, dc], target, own_sem.at[dc])
            else:
                copy = pltpu.make_async_remote_copy(
                    stage.at[dr, dc], target, row_send.at[dr, dc], row_recv.at[dr, dc],
                    device_id={"row": lax.rem(r - dr + rows, rows)}, device_id_type=MESH,
                )
            copy.start()
            copies.append(copy)
        return copies

    copies = pick(0)

    def prepare_one(b, carry):
        prepare(head_count, b, query_ref, lw_ref, lb_ref, samples_ref, point_s, corner_s)
        return carry

    lax.fori_loop(0, local_tiles, prepare_one, 0)

    def store(step, slab):
        return pltpu.make_async_copy(
            weight_s.at[slab], weights_ref.at[step // head_count, step % head_count],
            weight_sem.at[slab],
        )

    def weigh_one(step, carry):
        slab = step % 2

        @pl.when(step >= 2)
        def _():
            store(step - 2, slab).wait()

        weigh(sides, spans, per_block, step // head_count, step % head_count, slab,
              point_s, corner_s, mask_s, weight_s)
        store(step, slab).start()
        return carry

    steps = local_tiles * head_count
    done = 0
    for dc in range(1, cols):
        until = steps * dc // (cols - 1)
        if until > done:
            lax.fori_loop(done, until, weigh_one, 0)
        done = until
        col_copies[dc - 1].wait()
        copies += pick(dc)
    for step in range(max(0, steps - 2), steps):
        store(step, step % 2).wait()
    for copy in copies:
        copy.wait()


def mix_kernel(spans, per_block, head_count, head_dim, pos_ref, fetched_ref, upper_ref, lower_ref,
               out_ref,
               values, values_t, mixed, sem):
    block = pl.program_id(0)
    h = pl.program_id(1)
    blocks = pl.num_programs(0)

    def fetch(which):
        off = 0
        src = 0
        for level_num in range(LEVELS):
            span = spans[level_num]
            for k in range(per_block):
                pltpu.make_async_copy(
                    fetched_ref.at[pos_ref[level_num, which * per_block + k], pl.ds(src, span), :],
                    values.at[which % 2, pl.ds(off, span), :],
                    sem.at[which % 2],
                ).start()
                off += span
            src += span

    @pl.when((h == 0) & (block == 0))
    def _():
        fetch(block)

    @pl.when(h == 0)
    def _():
        side = block % 2
        pltpu.make_async_copy(values.at[side], values.at[side], sem.at[side]).wait()
        values_t[...] = values[side].T.reshape(values_t.shape)

        @pl.when(block + 1 < blocks)
        def _():
            fetch(block + 1)

    half = upper_ref.shape[2]
    mixed[h] = jnp.dot(
        values_t[h, :, :half], upper_ref[0, 0], preferred_element_type=jnp.float32
    ) + jnp.dot(values_t[h, :, half:], lower_ref[0, 0], preferred_element_type=jnp.float32)

    @pl.when(h == head_count - 1)
    def _():
        whole = mixed[...].reshape(head_count * head_dim, mixed.shape[2])
        out_ref[...] = whole.T.astype(jnp.bfloat16)


def on_device(
    queries,
    level_zero,
    level_one,
    level_two,
    level_three,
    tile_lists,
    samples,
    logit_weight,
    logit_bias,
    output_weight,
    output_bias,
    norm_gain,
    norm_shift,
):
    level_blocks = (level_zero, level_one, level_two, level_three)
    row_count = lax.axis_size("row")
    col_count = lax.axis_size("col")
    peer_count = row_count * col_count
    tile_rows, tile_cols, level_count, per_block = tile_lists.shape
    local_tiles = tile_rows * tile_cols
    requests = local_tiles * per_block
    capacity = max(2, (requests + peer_count - 1) // peer_count)
    slots = peer_count * capacity
    grid_cols = tile_cols * col_count
    channels = level_zero.shape[2]
    width_all = queries.shape[2]
    head_count = samples.shape[2] // (LEVELS * POINTS)
    head_dim = channels // head_count
    tile_side = level_zero.shape[0] // tile_rows
    pixels = tile_side * tile_side
    sides = [level_blocks[level_num].shape[0] // tile_rows for level_num in range(level_count)]
    spans = [max(PACK, side * side) for side in sides]
    tile_span = sum(spans)
    depth = per_block * tile_span

    wanted = tile_lists.transpose(2, 0, 1, 3).reshape(level_count, requests)
    grid_row = wanted // grid_cols
    grid_col = wanted % grid_cols
    owner_dev = grid_row // tile_rows * col_count + grid_col // tile_cols
    local_index = grid_row % tile_rows * tile_cols + grid_col % tile_cols
    order = jnp.arange(requests, dtype=jnp.int32)
    earlier = (owner_dev[:, :, None] == owner_dev[:, None, :]) & (order[None, :] < order[:, None])
    positions = owner_dev * capacity + jnp.sum(earlier.astype(jnp.int32), axis=2)
    slot_order = jnp.arange(slots, dtype=jnp.int32)
    named = positions[:, None, :] == slot_order[None, :, None]
    slot_table = jnp.max(jnp.where(named, local_index[:, None, :], -1), axis=2)
    table = jnp.maximum(slot_table, 0).reshape(level_count, row_count, col_count * capacity)
    table = table.transpose(1, 2, 0).reshape(row_count, col_count * capacity * level_count, 1)
    table_rows = table.shape[1]
    table = jnp.broadcast_to(table, (row_count, table_rows, channels))

    tiles_local = []
    for level_num in range(level_count):
        tiles = to_blocks(level_blocks[level_num], tile_rows, tile_cols, sides[level_num])
        short = spans[level_num] - tiles.shape[1]
        if short > 0:
            tiles = jnp.pad(tiles, ((0, 0), (0, short), (0, 0)))
        tiles_local.append(tiles.reshape(local_tiles * spans[level_num], channels))
    tiles_local = jnp.concatenate(tiles_local, axis=0)

    queries_blocked = to_blocks(queries, tile_rows, tile_cols, tile_side)
    samples_blocked = to_blocks(samples, tile_rows, tile_cols, tile_side)
    lanes = head_count * LEVELS * POINTS
    vmem = pl.BlockSpec(memory_space=pltpu.VMEM)
    whole = pl.BlockSpec(memory_space=pl.ANY)
    dma = pltpu.SemaphoreType.DMA
    fetched, weights = pl.pallas_call(
        functools.partial(exchange_kernel, sides, spans, per_block, head_count, row_count,
                          col_count, capacity, local_tiles),
        out_shape=(
            jax.ShapeDtypeStruct((slots, tile_span, channels), jnp.bfloat16),
            jax.ShapeDtypeStruct((local_tiles, head_count, depth, pixels), jnp.bfloat16),
        ),
        in_specs=[vmem] * 6,
        out_specs=(whole, whole),
        scratch_shapes=[
            pltpu.VMEM((local_tiles * tile_span, channels), jnp.bfloat16)
            for _ in range(col_count - 1)
        ] + [
            pltpu.VMEM((row_count, table_rows, channels), jnp.int32),
            pltpu.VMEM((row_count, col_count, capacity, tile_span, channels), jnp.bfloat16),
            pltpu.VMEM((local_tiles, 3, lanes, pixels), jnp.int32),
            pltpu.VMEM((local_tiles, 4, lanes, pixels), jnp.float32),
            pltpu.VMEM((POINTS * per_block, pixels), jnp.float32),
            pltpu.VMEM((2, depth, pixels), jnp.bfloat16),
            dma((row_count,)), dma((row_count,)), dma((col_count,)), dma((col_count,)),
            dma((row_count, col_count)), dma((row_count, col_count)), dma((col_count,)),
            dma, dma((2,)),
        ],
        compiler_params=pltpu.CompilerParams(
            collective_id=0, has_side_effects=True, vmem_limit_bytes=60 * 1024 * 1024
        ),
        cost_estimate=pl.CostEstimate(
            flops=8 * local_tiles * head_count * depth * pixels * POINTS,
            bytes_accessed=2 * local_tiles * head_count * depth * pixels, transcendentals=0,
        ),
        name="exchange",
    )(table, tiles_local, queries_blocked, logit_weight.T, logit_bias[:, None], samples_blocked)

    attn_out = pl.pallas_call(
        functools.partial(mix_kernel, spans, per_block, head_count, head_dim),
        grid_spec=pltpu.PrefetchScalarGridSpec(
            num_scalar_prefetch=1,
            grid=(local_tiles, head_count),
            in_specs=[
                pl.BlockSpec(memory_space=pl.ANY),
                pl.BlockSpec((1, 1, depth // 2, pixels), lambda b, h, pos: (b, h, 0, 0)),
                pl.BlockSpec((1, 1, depth // 2, pixels), lambda b, h, pos: (b, h, 1, 0)),
            ],
            out_specs=pl.BlockSpec((pixels, channels), lambda b, h, pos: (b, 0)),
            scratch_shapes=[
                pltpu.VMEM((2, depth, channels), jnp.bfloat16),
                pltpu.VMEM((head_count, head_dim, depth), jnp.bfloat16),
                pltpu.VMEM((head_count, head_dim, pixels), jnp.float32),
                pltpu.SemaphoreType.DMA((2,)),
            ],
        ),
        out_shape=jax.ShapeDtypeStruct((local_tiles * pixels, channels), jnp.bfloat16),
        compiler_params=pltpu.CompilerParams(
            dimension_semantics=("arbitrary", "arbitrary"), vmem_limit_bytes=60 * 1024 * 1024
        ),
        cost_estimate=pl.CostEstimate(
            flops=2 * local_tiles * depth * pixels * channels,
            bytes_accessed=2 * local_tiles * head_count * depth * pixels, transcendentals=0,
        ),
        name="mix",
    )(positions, fetched, weights, weights)

    head_index = lax.axis_index("head")
    full_attn = lax.all_gather(attn_out, "head", axis=1, tiled=True)
    pre_norm = (
        queries_blocked.reshape(local_tiles * pixels, width_all).astype(jnp.float32)
        + jnp.dot(full_attn, output_weight, preferred_element_type=jnp.float32)
        + output_bias
    )
    row_mean = jnp.mean(pre_norm, axis=1, keepdims=True)
    centered = pre_norm - row_mean
    variance = jnp.mean(centered * centered, axis=1, keepdims=True)
    own_part = lax.dynamic_slice_in_dim(centered, head_index * channels, channels, 1)
    normalized = own_part * lax.rsqrt(variance + 1e-05)
    updated = (normalized * norm_gain + norm_shift).astype(jnp.bfloat16)
    updated = updated.reshape(tile_rows, tile_cols, tile_side, tile_side, channels).transpose(
        0, 2, 1, 3, 4
    )
    return updated.reshape(tile_rows * tile_side, tile_cols * tile_side, channels)


def solution(mesh):
    in_specs = (
        P("row", "col", None),
        P("row", "col", "head"),
        P("row", "col", "head"),
        P("row", "col", "head"),
        P("row", "col", "head"),
        P("row", "col", None, None),
        P("row", "col", "head"),
        P(None, "head"),
        P("head"),
        P(),
        P(),
        P("head"),
        P("head"),
    )
    out_specs = P("row", "col", "head")
    return jax.shard_map(
        on_device, mesh=mesh, in_specs=in_specs, out_specs=out_specs, check_vma=False
    )
```

profile of v0, /device:TPU:25, one launch (start us, length us, event | category | flops | bytes accessed | tf_op | source)
XLA Modules:
  0.0 83.0 jit_solution(18260545726815025878)
XLA Ops:
  0.0 0.7 copy.20
  0.7 0.1 reshape.212
  0.9 0.2 convert_reduce_fusion
  1.1 0.1 select_reduce_fusion
  1.3 0.1 max.9
  1.3 0.1 copy.21
  1.4 0.1 broadcast_in_dim.20
  1.5 0.7 broadcast_in_dim.21.refs_0_
  2.3 0.7 pad.4
  2.9 1.8 %pad_maximum_fusion.refs_1_ = bf16[1408,128]{1,0:T(8,128)(2,1)} fusion(bf16[64,128]{1,0:T(8,128)(2,1)S(1)} %bitcast.22, bf16[64,128]{1,0:T(8,128)(2,1)} %bitcast.26, bf16[256,128]{1,0:T(8,128)(2,1)} %bitcast.23, bf16[1024,128]{1,0:T(8,128)(2,1)} %bitcast.21), kind=kLoop, calls=%fused_computation.5 | loop fusion | flops 1441792 | bytes 720896 | tf_op jit(solution)/shard_map/concatenate | solution.py:323
  4.7 1.3 %copy.22.refs_4_ = f32[64,1]{1,0:T(8,128)} copy(f32[64,1]{0,1:T(1,128)} %bitcast.29) | data formatting | bytes 512 | tf_op jit(solution)/shard_map/broadcast_in_dim | solution.py:362
  6.1 53.3 %exchange.1 = (bf16[32,352,128]{2,1,0:T(8,128)(2,1)}, bf16[4,4,2816,256]{3,2,1,0:T(8,128)(2,1)}) custom-call(s32[4,32,128]{2,1,0:T(8,128)} %broadcast_in_dim.21.refs_0_, bf16[1408,128]{1,0:T(8,128)(2,1)} %pad_maximum_fusion.refs_1_, bf16[4,256,256]{2,1,0:T(8,128)(2,1)} %bitcast.18, bf16[64,256]{1,0:T(8,128)(2,1)} %bitcast.24, f32[64,1]{1,0:T(8,128)} %copy.22.refs_4_, ...), custom_call_target="tpu_custom_call" | custom-call | flops 369098752 | bytes 23068672 | tf_op jit(solution)/shard_map/exchange/pallas_call | solution.py:331
  59.4 0.0 copy-done.2
  59.4 0.0 copy-start.1
  59.5 0.0 copy-start.3
  59.5 0.0 copy-start.4
  59.5 0.0 copy-start.5
  59.5 18.3 %mix.1 = bf16[1024,128]{1,0:T(8,128)(2,1)} custom-call(s32[4,32]{1,0:T(4,128)} %copy-done.2, bf16[32,352,128]{2,1,0:T(8,128)(2,1)} %get-tuple-element.7.fetched_ref, bf16[4,4,2816,256]{3,2,1,0:T(8,128)(2,1)} %get-tuple-element.8.upper_ref.lower_ref, bf16[4,4,2816,256]{3,2,1,0:T(8,128)(2,1)} %get-tuple-element.8.upper_ref.lower_ref), custom_call_target="tpu_custom_call" | custom-call | flops 738197504 | bytes 23068672 | tf_op jit(solution)/shard_map/mix/pallas_call | solution.py:364
  77.8 3.4 %all_gather.3 = bf16[1024,256]{1,0:T(8,128)(2,1)S(1)} all-gather(bf16[1024,128]{1,0:T(8,128)(2,1)} %mix.1), channel_id=1, replica_groups=mesh['row'=4,'col'=4,'head'=2] {'head'}, dimensions={1}, use_global_device_ids=true | all-gather | bytes 786432 | tf_op jit(solution)/shard_map/all_gather | solution.py:394
  81.2 0.0 copy-done
  81.2 0.0 copy-done.3
  81.2 0.4 fusion.5
  81.7 0.4 multiply_reduce_fusion
  82.1 0.9 %add_convert_fusion = bf16[1024,128]{1,0:T(8,128)(2,1)} fusion(f32[1024,256]{1,0:T(8,128)S(1)} %get-tuple-element.10, s32[]{:T(128)S(6)} %select_n.83, f32[128]{0:T(128)S(1)} %copy-done.4, f32[128]{0:T(128)S(1)} %copy-done.5, f32[1024]{0:T(1024)S(1)} %add_rsqrt_fusion), kind=kLoop, calls=%fused_computation.3 | loop fusion | flops 524288 | bytes 791556 | tf_op jit(solution)/shard_map/convert_element_type | solution.py:405
  (11 shorter events, 0.1 us)
Async XLA Ops:
  0.0 81.2 %copy-start = (bf16[256,256]{1,0:T(8,128)(2,1)S(1)}, bf16[256,256]{1,0:T(8,128)(2,1)}, u32[]{:S(2)}) copy-start(bf16[256,256]{1,0:T(8,128)(2,1)} %param.22) | copy-start | bytes 393220
  1.1 58.3 %copy-start.2 = (s32[4,32]{1,0:T(4,128)}, s32[4,32]{1,0:T(4,128)S(1)}, u32[]{:S(2)}) copy-start(s32[4,32]{1,0:T(4,128)S(1)} %multiply_add_fusion.pos_ref) | copy-start | bytes 1540
  59.4 21.8 %copy-start.1 = (bf16[64,16,256]{2,1,0:T(8,128)(2,1)S(1)}, bf16[64,16,256]{2,1,0:T(8,128)(2,1)}, u32[]{:S(2)}) copy-start(bf16[64,16,256]{2,1,0:T(8,128)(2,1)} %param.13) | copy-start | bytes 1572868
  59.5 21.8 %copy-start.3 = (f32[256]{0:T(256)S(1)}, f32[256]{0:T(256)}, u32[]{:S(2)}) copy-start(f32[256]{0:T(256)} %param.23) | copy-start | bytes 3076
  59.5 22.6 %copy-start.4 = (f32[128]{0:T(128)S(1)}, f32[128]{0:T(128)}, u32[]{:S(2)}) copy-start(f32[128]{0:T(128)} %param.25) | copy-start | bytes 1540
  59.5 22.6 %copy-start.5 = (f32[128]{0:T(128)S(1)}, f32[128]{0:T(128)}, u32[]{:S(2)}) copy-start(f32[128]{0:T(128)} %param.24) | copy-start | bytes 1540
where the time goes:
time: 83.6 us; the launch traced here: 83 us
  Pallas kernels  71.7 us (86%)
  local copies, waits for them, and re-layouts  3.88 us (5%)
  other arithmetic  3.49 us (4%)
  blocking collectives  3.41 us (4%)
    pallas_call x1, Pallas kernels, on_device(): pl.pallas_call(functools.partial(exchange_kernel, sides, spans, per_block...  53.3 us
    pallas_call x1, Pallas kernels, on_device(): pl.pallas_call(functools.partial(mix_kernel, spans, per_block, head_count...  18.3 us
    all_gather x1, blocking collectives, on_device(): full_attn = lax.all_gather(attn_out, 'head', axis=1, tiled=True)  3.41 us
    concatenate x1, other arithmetic, on_device(): tiles_local = jnp.concatenate(tiles_local, axis=0)  1.79 us

commit v1 on v0

--- a/solution.py
+++ b/solution.py
@@ -261,22 +261,7 @@
         out_ref[...] = whole.T.astype(jnp.bfloat16)
 
 
-def on_device(
-    queries,
-    level_zero,
-    level_one,
-    level_two,
-    level_three,
-    tile_lists,
-    samples,
-    logit_weight,
-    logit_bias,
-    output_weight,
-    output_bias,
-    norm_gain,
-    norm_shift,
-):
-    level_blocks = (level_zero, level_one, level_two, level_three)
+def gathered_attention(queries, level_blocks, tile_lists, samples, logit_weight, logit_bias, sides, spans):
     row_count = lax.axis_size("row")
     col_count = lax.axis_size("col")
     peer_count = row_count * col_count
@@ -286,14 +271,11 @@
     capacity = max(2, (requests + peer_count - 1) // peer_count)
     slots = peer_count * capacity
     grid_cols = tile_cols * col_count
-    channels = level_zero.shape[2]
-    width_all = queries.shape[2]
+    channels = level_blocks[0].shape[2]
     head_count = samples.shape[2] // (LEVELS * POINTS)
     head_dim = channels // head_count
-    tile_side = level_zero.shape[0] // tile_rows
+    tile_side = sides[0]
     pixels = tile_side * tile_side
-    sides = [level_blocks[level_num].shape[0] // tile_rows for level_num in range(level_count)]
-    spans = [max(PACK, side * side) for side in sides]
     tile_span = sum(spans)
     depth = per_block * tile_span
 
@@ -389,6 +371,492 @@
         ),
         name="mix",
     )(positions, fetched, weights, weights)
+    return attn_out
+
+
+def power_of_two(n):
+    return n > 0 and n & (n - 1) == 0
+
+
+def group_order(c, cols):
+    near = jnp.minimum(c, cols - 1 - c)
+    order = [c]
+    for g in range(1, cols):
+        both = c - (g + 1) // 2 if g % 2 else c + g // 2
+        one = jnp.where(c < cols - 1 - c, c + g - near, c - g + near)
+        order.append(jnp.where(g <= 2 * near, both, one))
+    return order
+
+
+def plan_tables(rows, cols, per_block, lists_ref, table, index_v):
+    blocks = lists_ref.shape[0]
+    wanted = jnp.concatenate([lists_ref[b] for b in range(blocks)], axis=1)
+    requests = wanted.shape[1]
+    tile_rows = blocks
+    col_bits = cols.bit_length() - 1
+    row_bits = tile_rows.bit_length() - 1
+    shape = (requests, requests)
+    down = lax.broadcasted_iota(jnp.int32, shape, 0)
+    along = lax.broadcasted_iota(jnp.int32, shape, 1)
+    capacity = requests // (rows * cols)
+    for level_num in range(LEVELS):
+        here = jnp.broadcast_to(wanted[level_num:level_num + 1, :], shape)
+        own_here = ((here >> (col_bits + row_bits)) << col_bits) + (here & (cols - 1))
+        local_here = (here >> col_bits) & (tile_rows - 1)
+        same = own_here == own_here.T
+        place_here = jnp.sum(jnp.where(same & (down < along), 1, 0), axis=0, keepdims=True)
+        slot_here = own_here * capacity + place_here
+        asked = jnp.sum(
+            jnp.where(slot_here == down, local_here.astype(jnp.float32), 0.0), axis=1, keepdims=True
+        )
+        asked = jnp.broadcast_to(asked, (requests, table.shape[3])).astype(jnp.int32)
+        table[:, level_num] = asked.reshape(rows, requests // rows, table.shape[3])
+        filled = jnp.sum(jnp.where(slot_here.T == along, down, 0), axis=0, keepdims=True)
+        index_v[level_num:level_num + 1, 0:requests] = filled
+
+
+def points(head_count, b, query_ref, lw_ref, bias, samples_ref, point_s, corner_s, slot_s):
+    queries_here = query_ref.shape[1]
+    hits = LEVELS * POINTS
+    logits = lax.dot_general(
+        lw_ref[...], query_ref[b], (((1,), (1,)), ((), ())), preferred_element_type=jnp.float32
+    ) + bias
+    logits = logits.reshape(head_count, hits, queries_here)
+    shifted = jnp.exp(logits - jnp.max(logits, axis=1, keepdims=True))
+    attend = shifted / jnp.sum(shifted, axis=1, keepdims=True)
+    attend = attend.reshape(head_count * hits, queries_here)
+    packed = samples_ref[b].T
+    pos_row = (packed >> 12) & 4095
+    pos_col = packed & 4095
+    frac_row = (pos_row & 255).astype(jnp.float32) * (1.0 / 256.0)
+    frac_col = (pos_col & 255).astype(jnp.float32) * (1.0 / 256.0)
+    point_s[b, 0] = pos_row >> 8
+    point_s[b, 1] = pos_col >> 8
+    corner_s[b, 0] = attend * (1.0 - frac_row)
+    corner_s[b, 1] = attend * frac_row
+    corner_s[b, 2] = 1.0 - frac_col
+    corner_s[b, 3] = frac_col
+    slot_s[b] = (packed >> 24).astype(jnp.float32)
+
+
+def spread(sides, spans, head_count, step, point_s, corner_s, spread_s):
+    hits = LEVELS * POINTS
+    queries_here = spread_s.shape[3]
+    b = step // head_count
+    h = step % head_count
+    half = PACK // 2
+    lane_row = lax.broadcasted_iota(jnp.int32, (PACK, queries_here), 0)
+    off = 0
+    for level_num in range(LEVELS):
+        side = sides[level_num]
+        span = spans[level_num]
+        for p in range(POINTS):
+            row = pl.ds(h * hits + level_num * POINTS + p, 1)
+            across = hat(lane_row % side, point_s[b, 1, row, :], corner_s[b, 2, row, :],
+                         corner_s[b, 3, row, :])
+            if side >= half:
+                wide = (half, queries_here)
+                start = jnp.broadcast_to(point_s[b, 0, row, :], wide)
+                low = jnp.broadcast_to(corner_s[b, 0, row, :], wide)
+                high = jnp.broadcast_to(corner_s[b, 1, row, :], wide)
+                downs = [hat(i, start, low, high) for i in range(side)]
+                for chunk in range(span // PACK):
+                    parts = []
+                    for part in range(2):
+                        at = chunk * PACK + part * half
+                        col = at % side
+                        if side == half:
+                            piece = across[part * half:(part + 1) * half, :]
+                        else:
+                            piece = across[col:col + half, :]
+                        parts.append(piece * downs[at // side])
+                    total = jnp.concatenate(parts, axis=0).astype(jnp.bfloat16)
+                    spread_s[step, p, off + chunk * PACK:off + (chunk + 1) * PACK, :] = total
+            else:
+                down = hat(lane_row // side, point_s[b, 0, row, :], corner_s[b, 0, row, :],
+                           corner_s[b, 1, row, :])
+                spread_s[step, p, off:off + PACK, :] = (across * down).astype(jnp.bfloat16)
+        off += span
+
+
+def weigh_slots(spans, per_block, head_count, rows, cols, group, index_s, slot_s, spread_s, weight_s):
+    hits = LEVELS * POINTS
+    queries_here = weight_s.shape[3]
+    capacity = 2
+    units = rows * capacity
+    block_bits = per_block.bit_length() - 1
+    requests = slot_s.shape[0] * per_block
+
+    def one(step, carry):
+        h = step // units
+        unit = step % units
+        slot = (unit // capacity * cols + group) * capacity + unit % capacity
+        off = 0
+        for level_num in range(LEVELS):
+            span = spans[level_num]
+            entry = index_s[level_num, slot] & (requests - 1)
+            b = entry >> block_bits
+            k = (entry & (per_block - 1)).astype(jnp.float32)
+            masks = []
+            for p in range(POINTS):
+                mine = slot_s[b, pl.ds(h * hits + level_num * POINTS + p, 1), :]
+                mine = jnp.broadcast_to(mine, (PACK, queries_here))
+                masks.append(jnp.where(mine == k, 1.0, 0.0).astype(jnp.bfloat16))
+            source = b * head_count + h
+            for chunk in range(span // PACK):
+                total = None
+                for p in range(POINTS):
+                    part = masks[p] * spread_s[source, p, off + chunk * PACK:off + (chunk + 1) * PACK, :]
+                    total = part if total is None else total + part
+                where = pl.multiple_of(units * off + unit * span + chunk * PACK, PACK)
+                weight_s[group, h, pl.ds(where, PACK), :] = total
+            off += span
+        return carry
+
+    lax.fori_loop(0, head_count * units, one, 0)
+
+
+def mix_slots(spans, per_block, head_count, head_dim, rows, cols, blocks, group, index_s, fetched,
+              turned, weight_s, mixed):
+    capacity = 2
+    units = rows * capacity
+    lanes = 128
+    block_bits = per_block.bit_length() - 1
+    turned[...] = fetched[group].T
+    lane = lax.broadcasted_iota(jnp.int32, (1, lanes), 1)
+    owners = []
+    off = 0
+    for level_num in range(LEVELS):
+        span = spans[level_num]
+        block_of = []
+        for unit in range(units):
+            slot = (unit // capacity * cols + group) * capacity + unit % capacity
+            block_of.append(index_s[level_num, slot] >> block_bits)
+        for start in range(0, units * span, lanes):
+            first = start // span
+            last = (start + lanes - 1) // span
+            value = jnp.full((1, lanes), block_of[first], jnp.int32)
+            for unit in range(first + 1, last + 1):
+                value = jnp.where(lane >= unit * span - start, block_of[unit], value)
+            owners.append(value)
+        off += span
+    owner_row = jnp.concatenate(owners, axis=1)
+    keep = [
+        jnp.broadcast_to(jnp.where(owner_row == b, 1.0, 0.0), (PACK, owner_row.shape[1])).astype(jnp.bfloat16)
+        for b in range(blocks)
+    ]
+    keep = [jnp.concatenate([one] * (head_dim // PACK), axis=0) for one in keep]
+
+    def one_head(h, carry):
+        base = turned[pl.ds(pl.multiple_of(h * head_dim, head_dim), head_dim), :]
+        left = jnp.concatenate([base * keep[b] for b in range(blocks)], axis=0)
+        mixed[h] += jnp.dot(left, weight_s[group, h], preferred_element_type=jnp.float32)
+        return carry
+
+    lax.fori_loop(0, head_count, one_head, 0)
+
+
+def fused_kernel(sides, spans, per_block, head_count, head_dim, rows, cols, *refs):
+    (lists_ref, zero_ref, one_ref, two_ref, three_ref, query_ref, lw_ref, lb_ref, samples_ref,
+     out_ref, blocks_v, table, ids_v, stage, fetched, index_v, index_s, point_s, corner_s, slot_s,
+     spread_s, weight_s, turned, mixed, id_send, id_recv, up_send, up_recv, down_send, down_recv,
+     row_send, row_recv, index_sem) = refs
+    levels = (zero_ref, one_ref, two_ref)
+    local_tiles = lists_ref.shape[0]
+    capacity = 2
+    r = lax.axis_index("row")
+    c = lax.axis_index("col")
+    lanes_wide = zero_ref.shape[1]
+    barrier = pltpu.get_barrier_semaphore()
+    for dr in range(1, rows):
+        pl.semaphore_signal(barrier, inc=1, device_id={"row": lax.rem(r + dr, rows)}, device_id_type=MESH)
+
+    @pl.when(c > 0)
+    def _():
+        pl.semaphore_signal(barrier, inc=1, device_id={"col": c - 1}, device_id_type=MESH)
+
+    @pl.when(c < cols - 1)
+    def _():
+        pl.semaphore_signal(barrier, inc=1, device_id={"col": c + 1}, device_id_type=MESH)
+
+    off = 0
+    for level_num in range(3):
+        size = local_tiles * spans[level_num]
+        blocks_v[c, off:off + size, :] = levels[level_num][...]
+        off += size
+    span = spans[3]
+    side = sides[3]
+    for tile in range(local_tiles):
+        rows_here = jnp.concatenate(
+            [three_ref[tile * side + i].astype(jnp.float32) for i in range(side)]
+            + [jnp.zeros((span - side * side, lanes_wide), jnp.float32)], axis=0
+        )
+        blocks_v[c, off + tile * span:off + (tile + 1) * span, :] = rows_here.astype(jnp.bfloat16)
+    plan_tables(rows, cols, per_block, lists_ref, table, index_v)
+
+    pl.semaphore_wait(barrier, rows - 1 + jnp.minimum(c, 1) + jnp.minimum(cols - 1 - c, 1))
+
+    block_rows = blocks_v.shape[1]
+    cuts = [0, 2 * spans[0], 4 * spans[0], block_rows]
+
+    def up(block, part):
+        at = blocks_v.at[block, pl.ds(cuts[part], cuts[part + 1] - cuts[part])]
+        return pltpu.make_async_remote_copy(
+            at, at, up_send.at[c - block, part], up_recv.at[c - block, part],
+            device_id={"col": c + 1}, device_id_type=MESH,
+        )
+
+    def down(block, part):
+        at = blocks_v.at[block, pl.ds(cuts[part], cuts[part + 1] - cuts[part])]
+        return pltpu.make_async_remote_copy(
+            at, at, down_send.at[block - c, part], down_recv.at[block - c, part],
+            device_id={"col": c - 1}, device_id_type=MESH,
+        )
+
+    def came_up(block, part):
+        at = blocks_v.at[block, pl.ds(cuts[part], cuts[part + 1] - cuts[part])]
+        return pltpu.make_async_remote_copy(
+            at, at, up_send.at[c - 1 - block, part], up_recv.at[c - 1 - block, part],
+            device_id={"col": c - 1}, device_id_type=MESH,
+        )
+
+    def came_down(block, part):
+        at = blocks_v.at[block, pl.ds(cuts[part], cuts[part + 1] - cuts[part])]
+        return pltpu.make_async_remote_copy(
+            at, at, down_send.at[block - c - 1, part], down_recv.at[block - c - 1, part],
+            device_id={"col": c + 1}, device_id_type=MESH,
+        )
+
+    parts = len(cuts) - 1
+    for part in range(parts):
+        @pl.when(c < cols - 1)
+        def _(part=part):
+            up(c, part).start()
+
+        @pl.when(c > 0)
+        def _(part=part):
+            down(c, part).start()
+
+    def id_copy(dr):
+        to = lax.rem(r + dr, rows)
+        return pltpu.make_async_remote_copy(
+            table.at[to], ids_v.at[dr], id_send.at[dr], id_recv.at[dr],
+            device_id={"row": to}, device_id_type=MESH,
+        )
+
+    for dr in range(1, rows):
+        id_copy(dr).start()
+    ids_v[0] = table[r]
+    bias = jnp.broadcast_to(lb_ref[...], (8, lb_ref.shape[1])).T[:, 0:1]
+
+    def points_one(b, carry):
+        points(head_count, b, query_ref, lw_ref, bias, samples_ref, point_s, corner_s, slot_s)
+        return carry
+
+    lax.fori_loop(0, local_tiles, points_one, 0)
+    index_copy = pltpu.make_async_copy(index_v, index_s, index_sem)
+    index_copy.start()
+    for dr in range(1, rows):
+        id_copy(dr).wait()
+
+    def arrive(block):
+        for part in range(parts):
+            @pl.when(block < c)
+            def _(part=part):
+                came_up(block, part).wait_recv()
+
+                @pl.when(c < cols - 1)
+                def _():
+                    up(block, part).start()
+
+            @pl.when(block > c)
+            def _(part=part):
+                came_down(block, part).wait_recv()
+
+                @pl.when(c > 0)
+                def _():
+                    down(block, part).start()
+
+    def row_copy(block, dr, level_num):
+        span = spans[level_num]
+        first = capacity * sum(spans[:level_num])
+        off = rows * first
+        size = capacity * span
+        return pltpu.make_async_remote_copy(
+            stage.at[block, dr - 1, pl.ds(first, size)],
+            fetched.at[block, pl.ds(pl.multiple_of(off + r * size, size), size)],
+            row_send.at[block, dr, level_num], row_recv.at[block, dr, level_num],
+            device_id={"row": lax.rem(r - dr + rows, rows)}, device_id_type=MESH,
+        )
+
+    def pick(block):
+        for turn in range(rows):
+            dr = (turn + 1) % rows
+            off = 0
+            for level_num in range(LEVELS):
+                span = spans[level_num]
+                size = capacity * span
+                for place in range(capacity):
+                    asked = jnp.broadcast_to(
+                        ids_v[dr, level_num, pl.ds(block * capacity + place, 1), :], (PACK, lanes_wide)
+                    )
+                    total = None
+                    for tile in range(local_tiles):
+                        mask = jnp.where(asked == tile, 1.0, 0.0).astype(jnp.bfloat16)
+                        first = local_tiles * off + tile * span
+                        part = blocks_v[block, first:first + span, :].reshape(
+                            span // PACK, PACK, lanes_wide) * mask[None]
+                        total = part if total is None else total + part
+                    total = total.reshape(span, lanes_wide)
+                    if dr == 0:
+                        at = pl.multiple_of(rows * capacity * off + r * size + place * span, span)
+                        fetched[block, pl.ds(at, span), :] = total
+                    else:
+                        at = capacity * off + place * span
+                        stage[block, dr - 1, at:at + span, :] = total
+                if dr != 0:
+                    row_copy(block, dr, level_num).start()
+                off += span
+
+    def settle(block):
+        for dr in range(1, rows):
+            for level_num in range(LEVELS):
+                row_copy(block, dr, level_num).wait_recv()
+
+    def spread_one(step, carry):
+        spread(sides, spans, head_count, step, point_s, corner_s, spread_s)
+        return carry
+
+    def weigh(block):
+        weigh_slots(spans, per_block, head_count, rows, cols, block, index_s, slot_s, spread_s, weight_s)
+
+    def mix(block):
+        settle(block)
+        mix_slots(spans, per_block, head_count, head_dim, rows, cols, local_tiles, block, index_s,
+                  fetched, turned, weight_s, mixed)
+
+    order = group_order(c, cols)
+    mixed[...] = jnp.zeros_like(mixed)
+    pick(order[0])
+    lax.fori_loop(0, local_tiles * head_count, spread_one, 0)
+    index_copy.wait()
+    for g in range(1, cols):
+        arrive(order[g])
+        pick(order[g])
+        weigh(order[g - 1])
+        if g > 1:
+            mix(order[g - 2])
+    weigh(order[cols - 1])
+    mix(order[cols - 2])
+    mix(order[cols - 1])
+
+    for b in range(local_tiles):
+        whole = mixed[:, b * head_dim:(b + 1) * head_dim, :].reshape(head_count * head_dim, mixed.shape[2])
+        size = mixed.shape[2]
+        out_ref[b * size:(b + 1) * size, :] = whole.T.astype(jnp.bfloat16)
+
+    for dr in range(1, rows):
+        for block in range(cols):
+            for level_num in range(LEVELS):
+                row_copy(block, dr, level_num).wait_send()
+    for block in range(cols):
+        for part in range(parts):
+            @pl.when((block <= c) & (c < cols - 1))
+            def _(block=block, part=part):
+                up(block, part).wait_send()
+
+            @pl.when((block >= c) & (c > 0))
+            def _(block=block, part=part):
+                down(block, part).wait_send()
+
+
+def fused_attention(queries, level_blocks, tile_lists, samples, logit_weight, logit_bias, sides, spans):
+    rows = lax.axis_size("row")
+    cols = lax.axis_size("col")
+    tile_rows, tile_cols, level_count, per_block = tile_lists.shape
+    local_tiles = tile_rows * tile_cols
+    requests = local_tiles * per_block
+    channels = level_blocks[0].shape[2]
+    lanes = samples.shape[2]
+    head_count = lanes // (LEVELS * POINTS)
+    head_dim = channels // head_count
+    pixels = spans[0]
+    tile_span = sum(spans)
+    capacity = requests // (rows * cols)
+    depth = rows * capacity * tile_span
+    flat = [level.reshape(-1, channels) for level in level_blocks[:3]]
+    vmem = pl.BlockSpec(memory_space=pltpu.VMEM)
+    dma = pltpu.SemaphoreType.DMA
+    parts = 3
+    return pl.pallas_call(
+        functools.partial(fused_kernel, sides, spans, per_block, head_count, head_dim, rows, cols),
+        out_shape=jax.ShapeDtypeStruct((local_tiles * pixels, channels), jnp.bfloat16),
+        in_specs=[vmem] * 9,
+        out_specs=vmem,
+        scratch_shapes=[
+            pltpu.VMEM((cols, local_tiles * tile_span, channels), jnp.bfloat16),
+            pltpu.VMEM((rows, LEVELS, requests // rows, channels), jnp.int32),
+            pltpu.VMEM((rows, LEVELS, requests // rows, channels), jnp.int32),
+            pltpu.VMEM((cols, rows - 1, capacity * tile_span, channels), jnp.bfloat16),
+            pltpu.VMEM((cols, depth, channels), jnp.bfloat16),
+            pltpu.VMEM((8, 128), jnp.int32),
+            pltpu.SMEM((8, 128), jnp.int32),
+            pltpu.VMEM((local_tiles, 2, lanes, pixels), jnp.int32),
+            pltpu.VMEM((local_tiles, 4, lanes, pixels), jnp.float32),
+            pltpu.VMEM((local_tiles, lanes, pixels), jnp.float32),
+            pltpu.VMEM((local_tiles * head_count, POINTS, tile_span, pixels), jnp.bfloat16),
+            pltpu.VMEM((cols, head_count, depth, pixels), jnp.bfloat16),
+            pltpu.VMEM((channels, depth), jnp.bfloat16),
+            pltpu.VMEM((head_count, local_tiles * head_dim, pixels), jnp.float32),
+            dma((rows,)), dma((rows,)),
+            dma((cols, parts)), dma((cols, parts)), dma((cols, parts)), dma((cols, parts)),
+            dma((cols, rows, LEVELS)), dma((cols, rows, LEVELS)),
+            dma,
+        ],
+        compiler_params=pltpu.CompilerParams(
+            collective_id=1, has_side_effects=True, vmem_limit_bytes=60 * 1024 * 1024
+        ),
+        name="fused",
+    )(
+        tile_lists.reshape(local_tiles, level_count, per_block), *flat, level_blocks[3],
+        queries.reshape(local_tiles, pixels, queries.shape[2]), logit_weight.T, logit_bias[None, :],
+        samples.reshape(local_tiles, pixels, lanes),
+    )
+
+
+def on_device(
+    queries,
+    level_zero,
+    level_one,
+    level_two,
+    level_three,
+    tile_lists,
+    samples,
+    logit_weight,
+    logit_bias,
+    output_weight,
+    output_bias,
+    norm_gain,
+    norm_shift,
+):
+    level_blocks = (level_zero, level_one, level_two, level_three)
+    tile_rows, tile_cols, level_count, per_block = tile_lists.shape
+    local_tiles = tile_rows * tile_cols
+    requests = local_tiles * per_block
+    channels = level_zero.shape[2]
+    width_all = queries.shape[2]
+    tile_side = level_zero.shape[0] // tile_rows
+    pixels = tile_side * tile_side
+    sides = [level.shape[0] // tile_rows for level in level_blocks]
+    spans = [max(PACK, side * side) for side in sides]
+    peer_count = lax.axis_size("row") * lax.axis_size("col")
+    full = requests == 2 * peer_count and tile_cols == 1 and sides == [16, 8, 4, 2]
+    full = full and all(power_of_two(n) for n in (tile_rows, lax.axis_size("col"), per_block))
+    attention = fused_attention if full else gathered_attention
+    attn_out = attention(
+        queries, level_blocks, tile_lists, samples, logit_weight, logit_bias, sides, spans
+    )
+    queries_blocked = to_blocks(queries, tile_rows, tile_cols, tile_side)
 
     head_index = lax.axis_index("head")
     full_attn = lax.all_gather(attn_out, "head", axis=1, tiled=True)

time: 83.6 us -> 55.8 us (0.67)
  the two profiles are of different devices: /device:TPU:25 before, /device:TPU:0 now
where the time goes in v1:
time: 55.8 us; the launch traced here: 55.6 us
  Pallas kernels  50 us (90%)
  blocking collectives  2.55 us (5%)
  local copies, waits for them, and re-layouts  1.33 us (2%)
  other arithmetic  1.28 us (2%)
    pallas_call x1, Pallas kernels, fused_attention(): pl.pallas_call(functools.partial(fused_kernel, sides, spans, per_block, h...  50 us
    all_gather x1, blocking collectives, on_device(): full_attn = lax.all_gather(attn_out, 'head', axis=1, tiled=True)  2.55 us
    unnamed x10, local copies, waits for them, and re-layouts  1.33 us

profile of v1, /device:TPU:0, one launch (start us, length us, event | category | flops | bytes accessed | tf_op | source)
XLA Modules:
  0.0 55.6 jit_solution(10428065663876801742)
XLA Ops:
  0.0 0.0 copy-start
  0.0 50.0 %fused.1 = bf16[1024,128]{1,0:T(8,128)(2,1)} custom-call(s32[4,4,8]{2,1,0:T(4,128)} %bitcast.20, bf16[1024,128]{1,0:T(8,128)(2,1)} %bitcast.16, bf16[256,128]{1,0:T(8,128)(2,1)} %bitcast.17, bf16[64,128]{1,0:T(8,128)(2,1)} %bitcast.19, bf16[8,2,128]{2,1,0:T(2,128)(2,1)} %refs_4_.1, bf16[4,256,256]{2,1,0:T(8,128)(2,1)} %bitcast.13, bf16[64,256]{1,0:T(8,128)(2,1)} %bitcast.18, ...), custom_call_target="tpu_custom_call" | custom-call | tf_op jit(solution)/shard_map/fused/pallas_call | solution.py:791
  50.0 0.0 copy-start.1
  50.0 2.6 %all_gather.3 = bf16[1024,256]{1,0:T(8,128)(2,1)S(1)} all-gather(bf16[1024,128]{1,0:T(8,128)(2,1)} %fused.1), channel_id=1, replica_groups=mesh['row'=4,'col'=4,'head'=2] {'head'}, dimensions={1}, use_global_device_ids=true | all-gather | bytes 786432 | tf_op jit(solution)/shard_map/all_gather | solution.py:862
  52.6 0.0 copy-start.2
  52.6 0.0 copy-done
  52.6 0.0 copy-done.1
  52.6 0.7 %copy-done.2 = f32[256]{0:T(256)S(1)} copy-done((f32[256]{0:T(256)S(1)}, f32[256]{0:T(256)}, u32[]{:S(2)}) %copy-start.2) | copy-done | bytes 1048
  53.3 0.4 fusion.1
  53.7 0.4 multiply_reduce_fusion
  54.1 0.0 copy-start.3
  54.1 0.0 copy-start.4
  54.1 0.6 %copy-done.3 = f32[128]{0:T(128)S(1)} copy-done((f32[128]{0:T(128)S(1)}, f32[128]{0:T(128)}, u32[]{:S(2)}) %copy-start.3) | copy-done | bytes 536
  54.7 0.0 copy-done.4
  54.7 0.9 %add_convert_fusion = bf16[1024,128]{1,0:T(8,128)(2,1)} fusion(f32[1024,256]{1,0:T(8,128)S(1)} %get-tuple-element.6, s32[]{:T(128)S(6)} %select_n.3, f32[128]{0:T(128)S(1)} %copy-done.3, f32[128]{0:T(128)S(1)} %copy-done.4, f32[1024]{0:T(1024)S(1)} %add_rsqrt_fusion), kind=kLoop, calls=%fused_computation.3 | loop fusion | flops 524288 | bytes 791556 | tf_op jit(solution)/shard_map/convert_element_type | solution.py:873
  (2 shorter events, 0.0 us)
Async XLA Ops:
  0.0 52.6 %copy-start = (bf16[256,256]{1,0:T(8,128)(2,1)S(1)}, bf16[256,256]{1,0:T(8,128)(2,1)}, u32[]{:S(2)}) copy-start(bf16[256,256]{1,0:T(8,128)(2,1)} %param.22) | copy-start | bytes 393220
  50.0 2.6 %copy-start.1 = (bf16[64,16,256]{2,1,0:T(8,128)(2,1)S(1)}, bf16[64,16,256]{2,1,0:T(8,128)(2,1)}, u32[]{:S(2)}) copy-start(bf16[64,16,256]{2,1,0:T(8,128)(2,1)} %param.13) | copy-start | bytes 1572868
  52.6 0.7 %copy-start.2 = (f32[256]{0:T(256)S(1)}, f32[256]{0:T(256)}, u32[]{:S(2)}) copy-start(f32[256]{0:T(256)} %param.23) | copy-start | bytes 3076
  54.1 0.7 %copy-start.3 = (f32[128]{0:T(128)S(1)}, f32[128]{0:T(128)}, u32[]{:S(2)}) copy-start(f32[128]{0:T(128)} %param.25) | copy-start | bytes 1540
  54.1 0.7 %copy-start.4 = (f32[128]{0:T(128)S(1)}, f32[128]{0:T(128)}, u32[]{:S(2)}) copy-start(f32[128]{0:T(128)} %param.24) | copy-start | bytes 1540

commit v2 on v1

--- a/solution.py
+++ b/solution.py
@@ -439,9 +439,18 @@
     slot_s[b] = (packed >> 24).astype(jnp.float32)
 
 
-def spread(sides, spans, head_count, step, point_s, corner_s, spread_s):
+def hats(start, low, high, count):
+    here = [start == i for i in range(count)]
+    out = [jnp.where(here[0], low, 0.0)]
+    for i in range(1, count):
+        out.append(jnp.where(here[i], low, jnp.where(here[i - 1], high, 0.0)))
+    return out
+
+
+def weigh_block(sides, spans, per_block, head_count, step, point_s, corner_s, slot_s, down_s, spread_s,
+                weight_s):
     hits = LEVELS * POINTS
-    queries_here = spread_s.shape[3]
+    queries_here = spread_s.shape[2]
     b = step // head_count
     h = step % head_count
     half = PACK // 2
@@ -454,84 +463,66 @@
             row = pl.ds(h * hits + level_num * POINTS + p, 1)
             across = hat(lane_row % side, point_s[b, 1, row, :], corner_s[b, 2, row, :],
                          corner_s[b, 3, row, :])
+            down = hat(lane_row // side if side < half else lane_row, point_s[b, 0, row, :],
+                       corner_s[b, 0, row, :], corner_s[b, 1, row, :])
             if side >= half:
-                wide = (half, queries_here)
-                start = jnp.broadcast_to(point_s[b, 0, row, :], wide)
-                low = jnp.broadcast_to(corner_s[b, 0, row, :], wide)
-                high = jnp.broadcast_to(corner_s[b, 1, row, :], wide)
-                downs = [hat(i, start, low, high) for i in range(side)]
+                at_down = (level_num * POINTS + p) * PACK
+                down_s[at_down:at_down + PACK, :] = down
                 for chunk in range(span // PACK):
                     parts = []
                     for part in range(2):
                         at = chunk * PACK + part * half
-                        col = at % side
-                        if side == half:
-                            piece = across[part * half:(part + 1) * half, :]
-                        else:
-                            piece = across[col:col + half, :]
-                        parts.append(piece * downs[at // side])
+                        col = at % side if side > half else part * half
+                        line = at_down + at // side
+                        parts.append(across[col:col + half, :] * down_s[line:line + 1, :])
                     total = jnp.concatenate(parts, axis=0).astype(jnp.bfloat16)
-                    spread_s[step, p, off + chunk * PACK:off + (chunk + 1) * PACK, :] = total
+                    spread_s[p, off + chunk * PACK:off + (chunk + 1) * PACK, :] = total
             else:
-                down = hat(lane_row // side, point_s[b, 0, row, :], corner_s[b, 0, row, :],
-                           corner_s[b, 1, row, :])
-                spread_s[step, p, off:off + PACK, :] = (across * down).astype(jnp.bfloat16)
+                spread_s[p, off:off + PACK, :] = (across * down).astype(jnp.bfloat16)
         off += span
-
-
-def weigh_slots(spans, per_block, head_count, rows, cols, group, index_s, slot_s, spread_s, weight_s):
-    hits = LEVELS * POINTS
-    queries_here = weight_s.shape[3]
-    capacity = 2
-    units = rows * capacity
-    block_bits = per_block.bit_length() - 1
-    requests = slot_s.shape[0] * per_block
-
-    def one(step, carry):
-        h = step // units
-        unit = step % units
-        slot = (unit // capacity * cols + group) * capacity + unit % capacity
-        off = 0
-        for level_num in range(LEVELS):
-            span = spans[level_num]
-            entry = index_s[level_num, slot] & (requests - 1)
-            b = entry >> block_bits
-            k = (entry & (per_block - 1)).astype(jnp.float32)
+    off = 0
+    quad = 4
+    one = jnp.ones((PACK, queries_here), jnp.bfloat16)
+    none = jnp.zeros((PACK, queries_here), jnp.bfloat16)
+    for level_num in range(LEVELS):
+        span = spans[level_num]
+        slots = []
+        for p in range(POINTS):
+            mine = slot_s[b, pl.ds(h * hits + level_num * POINTS + p, 1), :]
+            slots.append(jnp.broadcast_to(mine, (PACK, queries_here)).astype(jnp.bfloat16))
+        for first in range(0, per_block, quad):
             masks = []
-            for p in range(POINTS):
-                mine = slot_s[b, pl.ds(h * hits + level_num * POINTS + p, 1), :]
-                mine = jnp.broadcast_to(mine, (PACK, queries_here))
-                masks.append(jnp.where(mine == k, 1.0, 0.0).astype(jnp.bfloat16))
-            source = b * head_count + h
+            for k in range(first, first + quad):
+                label = jnp.full((PACK, queries_here), k, jnp.bfloat16)
+                masks.append([jnp.where(slots[p] == label, one, none) for p in range(POINTS)])
             for chunk in range(span // PACK):
-                total = None
-                for p in range(POINTS):
-                    part = masks[p] * spread_s[source, p, off + chunk * PACK:off + (chunk + 1) * PACK, :]
-                    total = part if total is None else total + part
-                where = pl.multiple_of(units * off + unit * span + chunk * PACK, PACK)
-                weight_s[group, h, pl.ds(where, PACK), :] = total
-            off += span
-        return carry
-
-    lax.fori_loop(0, head_count * units, one, 0)
+                pieces = [spread_s[p, off + chunk * PACK:off + (chunk + 1) * PACK, :] for p in range(POINTS)]
+                for k in range(first, first + quad):
+                    total = pieces[0] * masks[k - first][0]
+                    for p in range(1, POINTS):
+                        total = total + pieces[p] * masks[k - first][p]
+                    weight_s[level_num][step * per_block + k, chunk * PACK:(chunk + 1) * PACK, :] = total
+        off += span
 
 
 def mix_slots(spans, per_block, head_count, head_dim, rows, cols, blocks, group, index_s, fetched,
-              turned, weight_s, mixed):
+              turned, keep_s, weight_s, mixed, finish):
     capacity = 2
     units = rows * capacity
     lanes = 128
     block_bits = per_block.bit_length() - 1
+    requests = blocks * per_block
     turned[...] = fetched[group].T
     lane = lax.broadcasted_iota(jnp.int32, (1, lanes), 1)
+
+    def entry_of(level_num, unit):
+        slot = (unit // capacity * cols + group) * capacity + unit % capacity
+        return index_s[level_num, slot] & (requests - 1)
+
     owners = []
-    off = 0
     for level_num in range(LEVELS):
         span = spans[level_num]
-        block_of = []
-        for unit in range(units):
-            slot = (unit // capacity * cols + group) * capacity + unit % capacity
-            block_of.append(index_s[level_num, slot] >> block_bits)
+        block_of = [entry_of(level_num, unit) >> block_bits for unit in range(units)]
         for start in range(0, units * span, lanes):
             first = start // span
             last = (start + lanes - 1) // span
@@ -539,35 +530,61 @@
             for unit in range(first + 1, last + 1):
                 value = jnp.where(lane >= unit * span - start, block_of[unit], value)
             owners.append(value)
-        off += span
     owner_row = jnp.concatenate(owners, axis=1)
-    keep = [
-        jnp.broadcast_to(jnp.where(owner_row == b, 1.0, 0.0), (PACK, owner_row.shape[1])).astype(jnp.bfloat16)
-        for b in range(blocks)
-    ]
-    keep = [jnp.concatenate([one] * (head_dim // PACK), axis=0) for one in keep]
+    for b in range(blocks):
+        keep_s[b] = jnp.broadcast_to(
+            jnp.where(owner_row == b, 1.0, 0.0), (PACK, owner_row.shape[1])
+        ).astype(jnp.bfloat16)
 
     def one_head(h, carry):
-        base = turned[pl.ds(pl.multiple_of(h * head_dim, head_dim), head_dim), :]
-        left = jnp.concatenate([base * keep[b] for b in range(blocks)], axis=0)
-        mixed[h] += jnp.dot(left, weight_s[group, h], preferred_element_type=jnp.float32)
+        left = jnp.concatenate([
+            turned[pl.ds(pl.multiple_of(h * head_dim + half, PACK), PACK), :] * keep_s[b]
+            for b in range(blocks) for half in range(0, head_dim, PACK)
+        ], axis=0)
+        right = []
+        for level_num in range(LEVELS):
+            for unit in range(units):
+                entry = entry_of(level_num, unit)
+                source = (entry >> block_bits) * head_count + h
+                right.append(weight_s[level_num][source * per_block + (entry & (per_block - 1))])
+        right = jnp.concatenate(right, axis=0)
+        total = mixed[h] + jnp.dot(left, right, preferred_element_type=jnp.float32)
+        finish(h, total)
         return carry
 
     lax.fori_loop(0, head_count, one_head, 0)
 
 
 def fused_kernel(sides, spans, per_block, head_count, head_dim, rows, cols, *refs):
-    (lists_ref, zero_ref, one_ref, two_ref, three_ref, query_ref, lw_ref, lb_ref, samples_ref,
-     out_ref, blocks_v, table, ids_v, stage, fetched, index_v, index_s, point_s, corner_s, slot_s,
-     spread_s, weight_s, turned, mixed, id_send, id_recv, up_send, up_recv, down_send, down_recv,
-     row_send, row_recv, index_sem) = refs
-    levels = (zero_ref, one_ref, two_ref)
+    sources, refs = refs[:11], refs[11:]
+    out_ref, refs = refs[0], refs[1:]
+    held, refs = refs[:8], refs[8:]
+    (lists_ref, three_ref, query_ref, lw_ref, lb_ref, samples_ref, ow_ref, ob_ref) = held
+    (blocks_v, table, ids_v, stage, fetched, index_v, index_s, point_s,
+     corner_s, slot_s, down_s, spread_s, weight_0, weight_1, weight_2, weight_3, turned, keep_s, mixed,
+     attn_own, attn_other, id_send, id_recv, up_send, up_recv, down_send, down_recv, row_send, row_recv,
+     head_send, head_recv, index_sem, in_sem) = refs
+    weight_s = (weight_0, weight_1, weight_2, weight_3)
     local_tiles = lists_ref.shape[0]
     capacity = 2
     r = lax.axis_index("row")
     c = lax.axis_index("col")
-    lanes_wide = zero_ref.shape[1]
+    head = lax.axis_index("head")
+    lanes_wide = blocks_v.shape[2]
+    targets = []
+    off = 0
+    for level_num in range(3):
+        size = local_tiles * spans[level_num]
+        targets.append(blocks_v.at[c, pl.ds(off, size)])
+        off += size
+    loads = [
+        pltpu.make_async_copy(source, target, in_sem.at[i])
+        for i, (source, target) in enumerate(zip(sources, targets + list(held)))
+    ]
+    for load in loads:
+        load.start()
     barrier = pltpu.get_barrier_semaphore()
+    pl.semaphore_signal(barrier, inc=1, device_id={"head": 1 - head}, device_id_type=MESH)
     for dr in range(1, rows):
         pl.semaphore_signal(barrier, inc=1, device_id={"row": lax.rem(r + dr, rows)}, device_id_type=MESH)
 
@@ -579,11 +596,8 @@
     def _():
         pl.semaphore_signal(barrier, inc=1, device_id={"col": c + 1}, device_id_type=MESH)
 
-    off = 0
-    for level_num in range(3):
-        size = local_tiles * spans[level_num]
-        blocks_v[c, off:off + size, :] = levels[level_num][...]
-        off += size
+    for load in loads[3:5]:
+        load.wait()
     span = spans[3]
     side = sides[3]
     for tile in range(local_tiles):
@@ -594,7 +608,9 @@
         blocks_v[c, off + tile * span:off + (tile + 1) * span, :] = rows_here.astype(jnp.bfloat16)
     plan_tables(rows, cols, per_block, lists_ref, table, index_v)
 
-    pl.semaphore_wait(barrier, rows - 1 + jnp.minimum(c, 1) + jnp.minimum(cols - 1 - c, 1))
+    for load in loads[:3]:
+        load.wait()
+    pl.semaphore_wait(barrier, rows + jnp.minimum(c, 1) + jnp.minimum(cols - 1 - c, 1))
 
     block_rows = blocks_v.shape[1]
     cuts = [0, 2 * spans[0], 4 * spans[0], block_rows]
@@ -647,6 +663,8 @@
     for dr in range(1, rows):
         id_copy(dr).start()
     ids_v[0] = table[r]
+    for load in loads[5:]:
+        load.wait()
     bias = jnp.broadcast_to(lb_ref[...], (8, lb_ref.shape[1])).T[:, 0:1]
 
     def points_one(b, carry):
@@ -659,23 +677,24 @@
     for dr in range(1, rows):
         id_copy(dr).wait()
 
-    def arrive(block):
-        for part in range(parts):
-            @pl.when(block < c)
-            def _(part=part):
-                came_up(block, part).wait_recv()
-
-                @pl.when(c < cols - 1)
-                def _():
-                    up(block, part).start()
-
-            @pl.when(block > c)
-            def _(part=part):
-                came_down(block, part).wait_recv()
-
-                @pl.when(c > 0)
-                def _():
-                    down(block, part).start()
+    def relay(step, part):
+        @pl.when(c - 1 - step >= 0)
+        def _():
+            block = c - 1 - step
+            came_up(block, part).wait_recv()
+
+            @pl.when(c < cols - 1)
+            def _():
+                up(block, part).start()
+
+        @pl.when(c + 1 + step < cols)
+        def _():
+            block = c + 1 + step
+            came_down(block, part).wait_recv()
+
+            @pl.when(c > 0)
+            def _():
+                down(block, part).start()
 
     def row_copy(block, dr, level_num):
         span = spans[level_num]
@@ -723,37 +742,86 @@
             for level_num in range(LEVELS):
                 row_copy(block, dr, level_num).wait_recv()
 
-    def spread_one(step, carry):
-        spread(sides, spans, head_count, step, point_s, corner_s, spread_s)
-        return carry
-
-    def weigh(block):
-        weigh_slots(spans, per_block, head_count, rows, cols, block, index_s, slot_s, spread_s, weight_s)
-
-    def mix(block):
+    def weigh(first, last):
+        def one(step, carry):
+            weigh_block(sides, spans, per_block, head_count, step, point_s, corner_s, slot_s, down_s,
+                        spread_s, weight_s)
+            return carry
+
+        lax.fori_loop(first, last, one, 0)
+
+    def head_copy(h):
+        return pltpu.make_async_remote_copy(
+            attn_own.at[h], attn_other.at[h], head_send.at[h], head_recv.at[h],
+            device_id={"head": 1 - head}, device_id_type=MESH,
+        )
+
+    def keep_sum(h, total):
+        mixed[h] = total
+
+    def send_sum(h, total):
+        attn_own[h] = total.astype(jnp.bfloat16)
+        head_copy(h).start()
+
+    def mix(block, finish=keep_sum):
         settle(block)
         mix_slots(spans, per_block, head_count, head_dim, rows, cols, local_tiles, block, index_s,
-                  fetched, turned, weight_s, mixed)
+                  fetched, turned, keep_s, weight_s, mixed, finish)
 
     order = group_order(c, cols)
     mixed[...] = jnp.zeros_like(mixed)
     pick(order[0])
-    lax.fori_loop(0, local_tiles * head_count, spread_one, 0)
+    total_steps = local_tiles * head_count
+    early = total_steps * 5 // 8
     index_copy.wait()
-    for g in range(1, cols):
-        arrive(order[g])
+    for part in range(parts):
+        weigh(early * part // parts, early * (part + 1) // parts)
+        relay(0, part)
+    pick(order[1])
+    weigh(early, total_steps)
+    for g in range(2, cols):
+        for part in range(parts):
+            relay(g - 1, part)
+            if part == 0:
+                mix(order[g - 2])
         pick(order[g])
-        weigh(order[g - 1])
-        if g > 1:
-            mix(order[g - 2])
-    weigh(order[cols - 1])
     mix(order[cols - 2])
-    mix(order[cols - 1])
-
-    for b in range(local_tiles):
-        whole = mixed[:, b * head_dim:(b + 1) * head_dim, :].reshape(head_count * head_dim, mixed.shape[2])
-        size = mixed.shape[2]
-        out_ref[b * size:(b + 1) * size, :] = whole.T.astype(jnp.bfloat16)
+    mix(order[cols - 1], send_sum)
+
+    size = mixed.shape[2]
+    ch = head_count * head_dim
+    own_at = pl.multiple_of(head * ch, ch)
+    other_at = pl.multiple_of((1 - head) * ch, ch)
+    for h in range(head_count):
+        head_copy(h).wait()
+
+    def finish_block(b, carry):
+        here = pl.ds(pl.multiple_of(b * head_dim, head_dim), head_dim)
+        own = jnp.concatenate([attn_own[h, here, :] for h in range(head_count)], axis=0)
+        other = jnp.concatenate([attn_other[h, here, :] for h in range(head_count)], axis=0)
+
+        def project(at):
+            lanes = pl.ds(at, ch)
+            add = lax.dot_general(
+                own, ow_ref[pl.ds(own_at, ch), lanes], (((0,), (0,)), ((), ())),
+                preferred_element_type=jnp.float32,
+            ) + lax.dot_general(
+                other, ow_ref[pl.ds(other_at, ch), lanes], (((0,), (0,)), ((), ())),
+                preferred_element_type=jnp.float32,
+            )
+            return query_ref[b, :, lanes].astype(jnp.float32) + add + ob_ref[:, lanes]
+
+        mine = project(own_at)
+        rest = project(other_at)
+        scale = 1.0 / (2 * ch)
+        mean = jnp.sum(mine + rest, axis=1, keepdims=True) * scale
+        mine = mine - mean
+        rest = rest - mean
+        variance = jnp.sum(mine * mine + rest * rest, axis=1, keepdims=True) * scale
+        out_ref[pl.ds(pl.multiple_of(b * size, size), size), :] = mine * lax.rsqrt(variance + 1e-05)
+        return carry
+
+    lax.fori_loop(0, local_tiles, finish_block, 0)
 
     for dr in range(1, rows):
         for block in range(cols):
@@ -770,7 +838,8 @@
                 down(block, part).wait_send()
 
 
-def fused_attention(queries, level_blocks, tile_lists, samples, logit_weight, logit_bias, sides, spans):
+def fused_layer(queries, level_blocks, tile_lists, samples, logit_weight, logit_bias, output_weight,
+                output_bias, sides, spans):
     rows = lax.axis_size("row")
     cols = lax.axis_size("col")
     tile_rows, tile_cols, level_count, per_block = tile_lists.shape
@@ -785,15 +854,21 @@
     capacity = requests // (rows * cols)
     depth = rows * capacity * tile_span
     flat = [level.reshape(-1, channels) for level in level_blocks[:3]]
+    held = (
+        tile_lists.reshape(local_tiles, level_count, per_block), level_blocks[3],
+        queries.reshape(local_tiles, pixels, queries.shape[2]), logit_weight.T, logit_bias[None, :],
+        samples.reshape(local_tiles, pixels, lanes), output_weight, output_bias[None, :],
+    )
     vmem = pl.BlockSpec(memory_space=pltpu.VMEM)
     dma = pltpu.SemaphoreType.DMA
     parts = 3
     return pl.pallas_call(
         functools.partial(fused_kernel, sides, spans, per_block, head_count, head_dim, rows, cols),
-        out_shape=jax.ShapeDtypeStruct((local_tiles * pixels, channels), jnp.bfloat16),
-        in_specs=[vmem] * 9,
+        out_shape=jax.ShapeDtypeStruct((local_tiles * pixels, channels), jnp.float32),
+        in_specs=[pl.BlockSpec(memory_space=pltpu.HBM)] * 11,
         out_specs=vmem,
         scratch_shapes=[
+            *[pltpu.VMEM(one.shape, one.dtype) for one in held],
             pltpu.VMEM((cols, local_tiles * tile_span, channels), jnp.bfloat16),
             pltpu.VMEM((rows, LEVELS, requests // rows, channels), jnp.int32),
             pltpu.VMEM((rows, LEVELS, requests // rows, channels), jnp.int32),
@@ -804,24 +879,24 @@
             pltpu.VMEM((local_tiles, 2, lanes, pixels), jnp.int32),
             pltpu.VMEM((local_tiles, 4, lanes, pixels), jnp.float32),
             pltpu.VMEM((local_tiles, lanes, pixels), jnp.float32),
-            pltpu.VMEM((local_tiles * head_count, POINTS, tile_span, pixels), jnp.bfloat16),
-            pltpu.VMEM((cols, head_count, depth, pixels), jnp.bfloat16),
+            pltpu.VMEM((2 * POINTS * PACK, pixels), jnp.float32),
+            pltpu.VMEM((POINTS, tile_span, pixels), jnp.bfloat16),
+            *[pltpu.VMEM((local_tiles * head_count * per_block, span, pixels), jnp.bfloat16) for span in spans],
             pltpu.VMEM((channels, depth), jnp.bfloat16),
+            pltpu.VMEM((local_tiles, PACK, depth), jnp.bfloat16),
             pltpu.VMEM((head_count, local_tiles * head_dim, pixels), jnp.float32),
+            pltpu.VMEM((head_count, local_tiles * head_dim, pixels), jnp.bfloat16),
+            pltpu.VMEM((head_count, local_tiles * head_dim, pixels), jnp.bfloat16),
             dma((rows,)), dma((rows,)),
             dma((cols, parts)), dma((cols, parts)), dma((cols, parts)), dma((cols, parts)),
             dma((cols, rows, LEVELS)), dma((cols, rows, LEVELS)),
-            dma,
+            dma((head_count,)), dma((head_count,)), dma, dma((11,)),
         ],
         compiler_params=pltpu.CompilerParams(
-            collective_id=1, has_side_effects=True, vmem_limit_bytes=60 * 1024 * 1024
+            collective_id=1, has_side_effects=True, vmem_limit_bytes=44 * 1024 * 1024
         ),
         name="fused",
-    )(
-        tile_lists.reshape(local_tiles, level_count, per_block), *flat, level_blocks[3],
-        queries.reshape(local_tiles, pixels, queries.shape[2]), logit_weight.T, logit_bias[None, :],
-        samples.reshape(local_tiles, pixels, lanes),
-    )
+    )(*[pltpu.with_memory_space_constraint(one, pltpu.HBM) for one in (*flat, *held)])
 
 
 def on_device(
@@ -852,8 +927,15 @@
     peer_count = lax.axis_size("row") * lax.axis_size("col")
     full = requests == 2 * peer_count and tile_cols == 1 and sides == [16, 8, 4, 2]
     full = full and all(power_of_two(n) for n in (tile_rows, lax.axis_size("col"), per_block))
-    attention = fused_attention if full else gathered_attention
-    attn_out = attention(
+    full = full and lax.axis_size("head") == 2 and width_all == 2 * channels
+    if full:
+        updated = fused_layer(
+            queries, level_blocks, tile_lists, samples, logit_weight, logit_bias, output_weight,
+            output_bias, sides, spans
+        )
+        updated = (updated * norm_gain + norm_shift).astype(jnp.bfloat16)
+        return updated.reshape(tile_rows * tile_side, tile_cols * tile_side, channels)
+    attn_out = gathered_attention(
         queries, level_blocks, tile_lists, samples, logit_weight, logit_bias, sides, spans
     )
     queries_blocked = to_blocks(queries, tile_rows, tile_cols, tile_side)

time: 55.8 us -> 46.6 us (0.84)
  Pallas kernels: 50 us -> 45.6 us
  blocking collectives: 2.55 us -> 0 us
  local copies, waits for them, and re-layouts: 1.33 us -> 0.01 us
    pallas_call x1, Pallas kernels: 50 us -> 45.6 us  [fused_layer(): pl.pallas_call(functools.partial(fused_kernel, sides, spans, per_block, h...]
    all_gather x1 -> x0, blocking collectives: 2.55 us -> none  [on_device(): full_attn = lax.all_gather(attn_out, 'head', axis=1, tiled=True)]
    unnamed x10 -> x4, local copies, waits for them, and re-layouts: 1.33 us -> 0.01 us
where the time goes in v2:
time: 46.6 us; the launch traced here: 46.4 us
  Pallas kernels  45.6 us (98%)
  other arithmetic  0.76 us (2%)
    pallas_call x1, Pallas kernels, fused_layer(): pl.pallas_call(functools.partial(fused_kernel, sides, spans, per_block, h...  45.6 us

profile of v2, /device:TPU:0, one launch (start us, length us, event | category | flops | bytes accessed | tf_op | source)
XLA Modules:
  0.0 46.4 jit_solution(15672960913644935855)
XLA Ops:
  0.0 0.0 copy-start
  0.0 0.0 copy-start.1
  0.0 45.6 %fused.1 = f32[1024,128]{1,0:T(8,128)S(1)} custom-call(bf16[1024,128]{1,0:T(8,128)(2,1)} %bitcast.12, bf16[256,128]{1,0:T(8,128)(2,1)} %bitcast.13, bf16[64,128]{1,0:T(8,128)(2,1)} %bitcast.15, s32[4,4,8]{2,1,0:T(4,128)} %bitcast.16, bf16[8,2,128]{2,1,0:T(2,128)(2,1)} %refs_4_.1, bf16[4,256,256]{2,1,0:T(8,128)(2,1)} %bitcast.10, bf16[64,256]{1,0:T(8,128)(2,1)} %bitcast.14, ...), custom_call_target="tpu_custom_call" | custom-call | tf_op jit(solution)/shard_map/fused/pallas_call | solution.py:865
  45.6 0.0 copy-done
  45.7 0.0 copy-done.1
  45.7 0.8 %add_convert_fusion = bf16[1024,128]{1,0:T(8,128)(2,1)} fusion(f32[1024,128]{1,0:T(8,128)S(1)} %fused.1, f32[128]{0:T(128)S(1)} %copy-done, f32[128]{0:T(128)S(1)} %copy-done.1), kind=kLoop, calls=%fused_computation | loop fusion | flops 393216 | bytes 787456 | tf_op jit(solution)/shard_map/convert_element_type | solution.py:936
Async XLA Ops:
  0.0 45.6 %copy-start = (f32[128]{0:T(128)S(1)}, f32[128]{0:T(128)}, u32[]{:S(2)}) copy-start(f32[128]{0:T(128)} %param.25) | copy-start | bytes 1540
  0.0 45.7 %copy-start.1 = (f32[128]{0:T(128)S(1)}, f32[128]{0:T(128)}, u32[]{:S(2)}) copy-start(f32[128]{0:T(128)} %param.24) | copy-start | bytes 1540

commit v3 on v2

--- a/solution.py
+++ b/solution.py
@@ -10,6 +10,7 @@
 LEVELS = 4
 POINTS = 4
 PACK = 16
+TURNED = 1
 MESH = pl.DeviceIdType.MESH
 
 
@@ -388,7 +389,7 @@
     return order
 
 
-def plan_tables(rows, cols, per_block, lists_ref, table, index_v):
+def plan_tables(rows, cols, per_block, lists_ref, table, turned_table, index_v):
     blocks = lists_ref.shape[0]
     wanted = jnp.concatenate([lists_ref[b] for b in range(blocks)], axis=1)
     requests = wanted.shape[1]
@@ -401,7 +402,10 @@
     capacity = requests // (rows * cols)
     for level_num in range(LEVELS):
         here = jnp.broadcast_to(wanted[level_num:level_num + 1, :], shape)
-        own_here = ((here >> (col_bits + row_bits)) << col_bits) + (here & (cols - 1))
+        if level_num == TURNED:
+            own_here = (here & (cols - 1)) * rows + (here >> (col_bits + row_bits))
+        else:
+            own_here = ((here >> (col_bits + row_bits)) << col_bits) + (here & (cols - 1))
         local_here = (here >> col_bits) & (tile_rows - 1)
         same = own_here == own_here.T
         place_here = jnp.sum(jnp.where(same & (down < along), 1, 0), axis=0, keepdims=True)
@@ -410,7 +414,10 @@
             jnp.where(slot_here == down, local_here.astype(jnp.float32), 0.0), axis=1, keepdims=True
         )
         asked = jnp.broadcast_to(asked, (requests, table.shape[3])).astype(jnp.int32)
-        table[:, level_num] = asked.reshape(rows, requests // rows, table.shape[3])
+        if level_num == TURNED:
+            turned_table[...] = asked.reshape(turned_table.shape)
+        else:
+            table[:, level_num] = asked.reshape(rows, requests // rows, table.shape[3])
         filled = jnp.sum(jnp.where(slot_here.T == along, down, 0), axis=0, keepdims=True)
         index_v[level_num:level_num + 1, 0:requests] = filled
 
@@ -505,25 +512,32 @@
         off += span
 
 
-def mix_slots(spans, per_block, head_count, head_dim, rows, cols, blocks, group, index_s, fetched,
+def mix_slots(spans, per_block, head_count, head_dim, rows, cols, blocks, pieces, index_s, fetched,
               turned, keep_s, weight_s, mixed, finish):
     capacity = 2
     units = rows * capacity
     lanes = 128
     block_bits = per_block.bit_length() - 1
     requests = blocks * per_block
-    turned[...] = fetched[group].T
     lane = lax.broadcasted_iota(jnp.int32, (1, lanes), 1)
 
-    def entry_of(level_num, unit):
-        slot = (unit // capacity * cols + group) * capacity + unit % capacity
+    def entry_of(group, level_num, unit):
+        if level_num == TURNED:
+            slot = group * units + unit
+        else:
+            slot = (unit // capacity * cols + group) * capacity + unit % capacity
         return index_s[level_num, slot] & (requests - 1)
 
     owners = []
-    for level_num in range(LEVELS):
+    depth = 0
+    for group, level_num in pieces:
         span = spans[level_num]
-        block_of = [entry_of(level_num, unit) >> block_bits for unit in range(units)]
-        for start in range(0, units * span, lanes):
+        size = units * span
+        at = units * sum(spans[:level_num])
+        turned[:, depth:depth + size] = fetched[group, at:at + size, :].T
+        depth += size
+        block_of = [entry_of(group, level_num, unit) >> block_bits for unit in range(units)]
+        for start in range(0, size, lanes):
             first = start // span
             last = (start + lanes - 1) // span
             value = jnp.full((1, lanes), block_of[first], jnp.int32)
@@ -532,19 +546,20 @@
             owners.append(value)
     owner_row = jnp.concatenate(owners, axis=1)
     for b in range(blocks):
-        keep_s[b] = jnp.broadcast_to(
-            jnp.where(owner_row == b, 1.0, 0.0), (PACK, owner_row.shape[1])
+        keep_s[b, :, 0:depth] = jnp.broadcast_to(
+            jnp.where(owner_row == b, 1.0, 0.0), (PACK, depth)
         ).astype(jnp.bfloat16)
 
     def one_head(h, carry):
         left = jnp.concatenate([
-            turned[pl.ds(pl.multiple_of(h * head_dim + half, PACK), PACK), :] * keep_s[b]
+            turned[pl.ds(pl.multiple_of(h * head_dim + half, PACK), PACK), 0:depth]
+            * keep_s[b, :, 0:depth]
             for b in range(blocks) for half in range(0, head_dim, PACK)
         ], axis=0)
         right = []
-        for level_num in range(LEVELS):
+        for group, level_num in pieces:
             for unit in range(units):
-                entry = entry_of(level_num, unit)
+                entry = entry_of(group, level_num, unit)
                 source = (entry >> block_bits) * head_count + h
                 right.append(weight_s[level_num][source * per_block + (entry & (per_block - 1))])
         right = jnp.concatenate(right, axis=0)
@@ -560,10 +575,11 @@
     out_ref, refs = refs[0], refs[1:]
     held, refs = refs[:8], refs[8:]
     (lists_ref, three_ref, query_ref, lw_ref, lb_ref, samples_ref, ow_ref, ob_ref) = held
-    (blocks_v, table, ids_v, stage, fetched, index_v, index_s, point_s,
+    (layer_v, turned_table, turned_ids, turned_stage, blocks_v, table, ids_v, stage, fetched, index_v, index_s, point_s,
      corner_s, slot_s, down_s, spread_s, weight_0, weight_1, weight_2, weight_3, turned, keep_s, mixed,
      attn_own, attn_other, id_send, id_recv, up_send, up_recv, down_send, down_recv, row_send, row_recv,
-     head_send, head_recv, index_sem, in_sem) = refs
+     head_send, head_recv, layer_send, layer_recv, list_send, list_recv, turned_send, turned_recv,
+     index_sem, in_sem) = refs
     weight_s = (weight_0, weight_1, weight_2, weight_3)
     local_tiles = lists_ref.shape[0]
     capacity = 2
@@ -571,12 +587,17 @@
     c = lax.axis_index("col")
     head = lax.axis_index("head")
     lanes_wide = blocks_v.shape[2]
-    targets = []
+    starts = {}
     off = 0
-    for level_num in range(3):
-        size = local_tiles * spans[level_num]
-        targets.append(blocks_v.at[c, pl.ds(off, size)])
-        off += size
+    for level_num in range(LEVELS):
+        if level_num != TURNED:
+            starts[level_num] = off
+            off += local_tiles * spans[level_num]
+    targets = [
+        layer_v.at[r] if level_num == TURNED
+        else blocks_v.at[c, pl.ds(starts[level_num], local_tiles * spans[level_num])]
+        for level_num in range(3)
+    ]
     loads = [
         pltpu.make_async_copy(source, target, in_sem.at[i])
         for i, (source, target) in enumerate(zip(sources, targets + list(held)))
@@ -587,15 +608,8 @@
     pl.semaphore_signal(barrier, inc=1, device_id={"head": 1 - head}, device_id_type=MESH)
     for dr in range(1, rows):
         pl.semaphore_signal(barrier, inc=1, device_id={"row": lax.rem(r + dr, rows)}, device_id_type=MESH)
-
-    @pl.when(c > 0)
-    def _():
-        pl.semaphore_signal(barrier, inc=1, device_id={"col": c - 1}, device_id_type=MESH)
-
-    @pl.when(c < cols - 1)
-    def _():
-        pl.semaphore_signal(barrier, inc=1, device_id={"col": c + 1}, device_id_type=MESH)
-
+    for dc in range(1, cols):
+        pl.semaphore_signal(barrier, inc=1, device_id={"col": lax.rem(c + dc, cols)}, device_id_type=MESH)
     for load in loads[3:5]:
         load.wait()
     span = spans[3]
@@ -605,45 +619,83 @@
             [three_ref[tile * side + i].astype(jnp.float32) for i in range(side)]
             + [jnp.zeros((span - side * side, lanes_wide), jnp.float32)], axis=0
         )
-        blocks_v[c, off + tile * span:off + (tile + 1) * span, :] = rows_here.astype(jnp.bfloat16)
-    plan_tables(rows, cols, per_block, lists_ref, table, index_v)
+        at = starts[3] + tile * span
+        blocks_v[c, at:at + span, :] = rows_here.astype(jnp.bfloat16)
+    plan_tables(rows, cols, per_block, lists_ref, table, turned_table, index_v)
 
     for load in loads[:3]:
         load.wait()
-    pl.semaphore_wait(barrier, rows + jnp.minimum(c, 1) + jnp.minimum(cols - 1 - c, 1))
+    pl.semaphore_wait(barrier, rows + cols - 1)
 
     block_rows = blocks_v.shape[1]
-    cuts = [0, 2 * spans[0], 4 * spans[0], block_rows]
+    parts = 3
+    part_rows = block_rows // parts
 
     def up(block, part):
-        at = blocks_v.at[block, pl.ds(cuts[part], cuts[part + 1] - cuts[part])]
+        at = blocks_v.at[block, pl.ds(pl.multiple_of(part * part_rows, PACK), part_rows)]
         return pltpu.make_async_remote_copy(
             at, at, up_send.at[c - block, part], up_recv.at[c - block, part],
             device_id={"col": c + 1}, device_id_type=MESH,
         )
 
     def down(block, part):
-        at = blocks_v.at[block, pl.ds(cuts[part], cuts[part + 1] - cuts[part])]
+        at = blocks_v.at[block, pl.ds(pl.multiple_of(part * part_rows, PACK), part_rows)]
         return pltpu.make_async_remote_copy(
             at, at, down_send.at[block - c, part], down_recv.at[block - c, part],
             device_id={"col": c - 1}, device_id_type=MESH,
         )
 
     def came_up(block, part):
-        at = blocks_v.at[block, pl.ds(cuts[part], cuts[part + 1] - cuts[part])]
+        at = blocks_v.at[block, pl.ds(pl.multiple_of(part * part_rows, PACK), part_rows)]
         return pltpu.make_async_remote_copy(
             at, at, up_send.at[c - 1 - block, part], up_recv.at[c - 1 - block, part],
             device_id={"col": c - 1}, device_id_type=MESH,
         )
 
     def came_down(block, part):
-        at = blocks_v.at[block, pl.ds(cuts[part], cuts[part + 1] - cuts[part])]
+        at = blocks_v.at[block, pl.ds(pl.multiple_of(part * part_rows, PACK), part_rows)]
         return pltpu.make_async_remote_copy(
             at, at, down_send.at[block - c - 1, part], down_recv.at[block - c - 1, part],
             device_id={"col": c + 1}, device_id_type=MESH,
         )
 
-    parts = len(cuts) - 1
+    def id_copy(dr):
+        to = lax.rem(r + dr, rows)
+        return pltpu.make_async_remote_copy(
+            table.at[to], ids_v.at[dr], id_send.at[dr], id_recv.at[dr],
+            device_id={"row": to}, device_id_type=MESH,
+        )
+
+    def list_copy(dc):
+        to = lax.rem(c + dc, cols)
+        return pltpu.make_async_remote_copy(
+            turned_table.at[to], turned_ids.at[c], list_send.at[dc], list_recv.at[dc],
+            device_id={"col": to}, device_id_type=MESH,
+        )
+
+    def layer_copy(dr):
+        return pltpu.make_async_remote_copy(
+            layer_v.at[r], layer_v.at[r], layer_send.at[dr], layer_recv.at[dr],
+            device_id={"row": lax.rem(r + dr, rows)}, device_id_type=MESH,
+        )
+
+    def layer_came(dr):
+        at = layer_v.at[lax.rem(r - dr + rows, rows)]
+        return pltpu.make_async_remote_copy(
+            at, at, layer_send.at[dr], layer_recv.at[dr],
+            device_id={"row": lax.rem(r + dr, rows)}, device_id_type=MESH,
+        )
+
+    def list_came(dc):
+        return pltpu.make_async_remote_copy(
+            turned_table.at[c], turned_ids.at[lax.rem(c - dc + cols, cols)], list_send.at[dc],
+            list_recv.at[dc], device_id={"col": lax.rem(c + dc, cols)}, device_id_type=MESH,
+        )
+
+    for dr in range(1, rows):
+        id_copy(dr).start()
+    for dc in range(1, cols):
+        list_copy(dc).start()
     for part in range(parts):
         @pl.when(c < cols - 1)
         def _(part=part):
@@ -653,15 +705,9 @@
         def _(part=part):
             down(c, part).start()
 
-    def id_copy(dr):
-        to = lax.rem(r + dr, rows)
-        return pltpu.make_async_remote_copy(
-            table.at[to], ids_v.at[dr], id_send.at[dr], id_recv.at[dr],
-            device_id={"row": to}, device_id_type=MESH,
-        )
-
     for dr in range(1, rows):
-        id_copy(dr).start()
+        layer_copy(dr).start()
+    turned_ids[c] = turned_table[c]
     ids_v[0] = table[r]
     for load in loads[5:]:
         load.wait()
@@ -715,6 +761,9 @@
             for level_num in range(LEVELS):
                 span = spans[level_num]
                 size = capacity * span
+                if level_num == TURNED:
+                    off += span
+                    continue
                 for place in range(capacity):
                     asked = jnp.broadcast_to(
                         ids_v[dr, level_num, pl.ds(block * capacity + place, 1), :], (PACK, lanes_wide)
@@ -722,7 +771,7 @@
                     total = None
                     for tile in range(local_tiles):
                         mask = jnp.where(asked == tile, 1.0, 0.0).astype(jnp.bfloat16)
-                        first = local_tiles * off + tile * span
+                        first = starts[level_num] + tile * span
                         part = blocks_v[block, first:first + span, :].reshape(
                             span // PACK, PACK, lanes_wide) * mask[None]
                         total = part if total is None else total + part
@@ -737,10 +786,43 @@
                     row_copy(block, dr, level_num).start()
                 off += span
 
+    turned_span = spans[TURNED]
+    turned_at = rows * capacity * sum(spans[:TURNED])
+    turned_size = rows * capacity * turned_span
+
+    def turned_copy(block, to):
+        return pltpu.make_async_remote_copy(
+            turned_stage.at[to], fetched.at[block, pl.ds(turned_at, turned_size)],
+            turned_send.at[to], turned_recv.at[block],
+            device_id={"col": to}, device_id_type=MESH,
+        )
+
+    def pick_turned(to, target, base):
+        for owner in range(rows):
+            for place in range(capacity):
+                unit = owner * capacity + place
+                asked = jnp.broadcast_to(turned_ids[to, pl.ds(unit, 1), :], (PACK, lanes_wide))
+                total = None
+                for tile in range(local_tiles):
+                    mask = jnp.where(asked == tile, 1.0, 0.0).astype(jnp.bfloat16)
+                    part = layer_v[owner, tile * turned_span:(tile + 1) * turned_span, :].reshape(
+                        turned_span // PACK, PACK, lanes_wide) * mask[None]
+                    total = part if total is None else total + part
+                at = base + unit * turned_span
+                target[at:at + turned_span, :] = total.reshape(turned_span, lanes_wide)
+
+    def send_turned(step):
+        for to, before in ((step + 1, True), (cols - 2 - step, False)):
+            @pl.when(c < to if before else c > to)
+            def _(to=to):
+                pick_turned(to, turned_stage.at[to], 0)
+                turned_copy(c, to).start()
+
     def settle(block):
         for dr in range(1, rows):
             for level_num in range(LEVELS):
-                row_copy(block, dr, level_num).wait_recv()
+                if level_num != TURNED:
+                    row_copy(block, dr, level_num).wait_recv()
 
     def weigh(first, last):
         def one(step, carry):
@@ -763,30 +845,49 @@
         attn_own[h] = total.astype(jnp.bfloat16)
         head_copy(h).start()
 
-    def mix(block, finish=keep_sum):
+    straight = [level_num for level_num in range(LEVELS) if level_num != TURNED]
+
+    def mix(pieces, finish=keep_sum):
+        mix_slots(spans, per_block, head_count, head_dim, rows, cols, local_tiles, pieces, index_s,
+                  fetched, turned, keep_s, weight_s, mixed, finish)
+
+    def mix_straight(block, finish=keep_sum):
         settle(block)
-        mix_slots(spans, per_block, head_count, head_dim, rows, cols, local_tiles, block, index_s,
-                  fetched, turned, keep_s, weight_s, mixed, finish)
+        mix([(block, level_num) for level_num in straight], finish)
 
     order = group_order(c, cols)
     mixed[...] = jnp.zeros_like(mixed)
     pick(order[0])
     total_steps = local_tiles * head_count
-    early = total_steps * 5 // 8
     index_copy.wait()
-    for part in range(parts):
-        weigh(early * part // parts, early * (part + 1) // parts)
-        relay(0, part)
-    pick(order[1])
-    weigh(early, total_steps)
-    for g in range(2, cols):
-        for part in range(parts):
-            relay(g - 1, part)
-            if part == 0:
-                mix(order[g - 2])
+
+    def relay_and_weigh(step, share):
+        def one(part, carry):
+            first = (step * parts + part) * share
+            weigh(jnp.minimum(first, total_steps), jnp.minimum(first + share, total_steps))
+            relay(step, part)
+            return carry
+
+        lax.fori_loop(0, parts, one, 0)
+
+    for g in range(1, cols):
+        relay_and_weigh(g - 1, -(-total_steps // (parts * (cols - 1))))
         pick(order[g])
-    mix(order[cols - 2])
-    mix(order[cols - 1], send_sum)
+        if g == 1:
+            for dr in range(1, rows):
+                layer_came(dr).wait_recv()
+            for dc in range(1, cols):
+                list_came(dc).wait_recv()
+            pick_turned(c, fetched.at[c], turned_at)
+        send_turned(g - 1)
+    settle(order[0])
+    mix([(order[0], level_num) for level_num in range(LEVELS)])
+    for g in range(1, cols - 1):
+        mix_straight(order[g])
+    for g in range(1, cols):
+        turned_copy(order[g], order[g]).wait_recv()
+    mix([(order[g], TURNED) for g in range(1, cols)])
+    mix_straight(order[cols - 1], send_sum)
 
     size = mixed.shape[2]
     ch = head_count * head_dim
@@ -824,9 +925,14 @@
     lax.fori_loop(0, local_tiles, finish_block, 0)
 
     for dr in range(1, rows):
+        layer_copy(dr).wait_send()
         for block in range(cols):
             for level_num in range(LEVELS):
-                row_copy(block, dr, level_num).wait_send()
+                if level_num != TURNED:
+                    row_copy(block, dr, level_num).wait_send()
+    for dc in range(1, cols):
+        list_copy(dc).wait_send()
+        turned_copy(c, lax.rem(c + dc, cols)).wait_send()
     for block in range(cols):
         for part in range(parts):
             @pl.when((block <= c) & (c < cols - 1))
@@ -869,7 +975,11 @@
         out_specs=vmem,
         scratch_shapes=[
             *[pltpu.VMEM(one.shape, one.dtype) for one in held],
-            pltpu.VMEM((cols, local_tiles * tile_span, channels), jnp.bfloat16),
+            pltpu.VMEM((rows, local_tiles * spans[TURNED], channels), jnp.bfloat16),
+            pltpu.VMEM((cols, requests // cols, channels), jnp.int32),
+            pltpu.VMEM((cols, requests // cols, channels), jnp.int32),
+            pltpu.VMEM((cols, rows * capacity * spans[TURNED], channels), jnp.bfloat16),
+            pltpu.VMEM((cols, local_tiles * (tile_span - spans[TURNED]), channels), jnp.bfloat16),
             pltpu.VMEM((rows, LEVELS, requests // rows, channels), jnp.int32),
             pltpu.VMEM((rows, LEVELS, requests // rows, channels), jnp.int32),
             pltpu.VMEM((cols, rows - 1, capacity * tile_span, channels), jnp.bfloat16),
@@ -890,7 +1000,8 @@
             dma((rows,)), dma((rows,)),
             dma((cols, parts)), dma((cols, parts)), dma((cols, parts)), dma((cols, parts)),
             dma((cols, rows, LEVELS)), dma((cols, rows, LEVELS)),
-            dma((head_count,)), dma((head_count,)), dma, dma((11,)),
+            dma((head_count,)), dma((head_count,)), dma((rows,)), dma((rows,)),
+            dma((cols,)), dma((cols,)), dma((cols,)), dma((cols,)), dma, dma((11,)),
         ],
         compiler_params=pltpu.CompilerParams(
             collective_id=1, has_side_effects=True, vmem_limit_bytes=44 * 1024 * 1024

time: 46.6 us -> 44.1 us (0.946)
  Pallas kernels: 45.6 us -> 43.1 us
    pallas_call x1, Pallas kernels: 45.6 us -> 43.1 us  [fused_layer(): pl.pallas_call(functools.partial(fused_kernel, sides, spans, per_block, h...]
where the time goes in v3:
time: 44.1 us; the launch traced here: 43.9 us
  Pallas kernels  43.1 us (98%)
  other arithmetic  0.76 us (2%)
    pallas_call x1, Pallas kernels, fused_layer(): pl.pallas_call(functools.partial(fused_kernel, sides, spans, per_block, h...  43.1 us

profile of v3, /device:TPU:0, one launch (start us, length us, event | category | flops | bytes accessed | tf_op | source)
XLA Modules:
  0.0 43.9 jit_solution(12408468953605513819)
XLA Ops:
  0.0 0.0 copy-start
  0.0 0.0 copy-start.1
  0.0 43.1 %fused.1 = f32[1024,128]{1,0:T(8,128)S(1)} custom-call(bf16[1024,128]{1,0:T(8,128)(2,1)} %bitcast.12, bf16[256,128]{1,0:T(8,128)(2,1)} %bitcast.13, bf16[64,128]{1,0:T(8,128)(2,1)} %bitcast.15, s32[4,4,8]{2,1,0:T(4,128)} %bitcast.16, bf16[8,2,128]{2,1,0:T(2,128)(2,1)} %refs_4_.1, bf16[4,256,256]{2,1,0:T(8,128)(2,1)} %bitcast.10, bf16[64,256]{1,0:T(8,128)(2,1)} %bitcast.14, ...), custom_call_target="tpu_custom_call" | custom-call | tf_op jit(solution)/shard_map/fused/pallas_call | solution.py:971
  43.1 0.0 copy-done
  43.2 0.0 copy-done.1
  43.2 0.8 %add_convert_fusion = bf16[1024,128]{1,0:T(8,128)(2,1)} fusion(f32[1024,128]{1,0:T(8,128)S(1)} %fused.1, f32[128]{0:T(128)S(1)} %copy-done, f32[128]{0:T(128)S(1)} %copy-done.1), kind=kLoop, calls=%fused_computation | loop fusion | flops 393216 | bytes 787456 | tf_op jit(solution)/shard_map/convert_element_type | solution.py:1047
Async XLA Ops:
  0.0 43.1 %copy-start = (f32[128]{0:T(128)S(1)}, f32[128]{0:T(128)}, u32[]{:S(2)}) copy-start(f32[128]{0:T(128)} %param.25) | copy-start | bytes 1540
  0.0 43.2 %copy-start.1 = (f32[128]{0:T(128)S(1)}, f32[128]{0:T(128)}, u32[]{:S(2)}) copy-start(f32[128]{0:T(128)} %param.24) | copy-start | bytes 1540

commit v4 on v3

--- a/solution.py
+++ b/solution.py
@@ -571,10 +571,11 @@
 
 
 def fused_kernel(sides, spans, per_block, head_count, head_dim, rows, cols, *refs):
-    sources, refs = refs[:11], refs[11:]
+    sources, refs = refs[:13], refs[13:]
     out_ref, refs = refs[0], refs[1:]
-    held, refs = refs[:8], refs[8:]
-    (lists_ref, three_ref, query_ref, lw_ref, lb_ref, samples_ref, ow_ref, ob_ref) = held
+    held, refs = refs[:10], refs[10:]
+    (lists_ref, three_ref, query_ref, lw_ref, lb_ref, samples_ref, ow_ref, ob_ref,
+     gain_ref, shift_ref) = held
     (layer_v, turned_table, turned_ids, turned_stage, blocks_v, table, ids_v, stage, fetched, index_v, index_s, point_s,
      corner_s, slot_s, down_s, spread_s, weight_0, weight_1, weight_2, weight_3, turned, keep_s, mixed,
      attn_own, attn_other, id_send, id_recv, up_send, up_recv, down_send, down_recv, row_send, row_recv,
@@ -592,7 +593,7 @@
     for level_num in range(LEVELS):
         if level_num != TURNED:
             starts[level_num] = off
-            off += local_tiles * spans[level_num]
+            off += local_tiles * (spans[level_num] if level_num < LEVELS - 1 else PACK // 2)
     targets = [
         layer_v.at[r] if level_num == TURNED
         else blocks_v.at[c, pl.ds(starts[level_num], local_tiles * spans[level_num])]
@@ -612,7 +613,7 @@
         pl.semaphore_signal(barrier, inc=1, device_id={"col": lax.rem(c + dc, cols)}, device_id_type=MESH)
     for load in loads[3:5]:
         load.wait()
-    span = spans[3]
+    span = PACK // 2
     side = sides[3]
     for tile in range(local_tiles):
         rows_here = jnp.concatenate(
@@ -621,6 +622,9 @@
         )
         at = starts[3] + tile * span
         blocks_v[c, at:at + span, :] = rows_here.astype(jnp.bfloat16)
+    depth = fetched.shape[1]
+    padded = rows * capacity * spans[3]
+    fetched[:, depth - padded:depth, :] = jnp.zeros((cols, padded, lanes_wide), jnp.bfloat16)
     plan_tables(rows, cols, per_block, lists_ref, table, turned_table, index_v)
 
     for load in loads[:3]:
@@ -628,7 +632,7 @@
     pl.semaphore_wait(barrier, rows + cols - 1)
 
     block_rows = blocks_v.shape[1]
-    parts = 3
+    parts = 2
     part_rows = block_rows // parts
 
     def up(block, part):
@@ -720,9 +724,6 @@
     lax.fori_loop(0, local_tiles, points_one, 0)
     index_copy = pltpu.make_async_copy(index_v, index_s, index_sem)
     index_copy.start()
-    for dr in range(1, rows):
-        id_copy(dr).wait()
-
     def relay(step, part):
         @pl.when(c - 1 - step >= 0)
         def _():
@@ -742,21 +743,31 @@
             def _():
                 down(block, part).start()
 
+    half = PACK // 2
+    last = LEVELS - 1
+
     def row_copy(block, dr, level_num):
-        span = spans[level_num]
-        first = capacity * sum(spans[:level_num])
-        off = rows * first
+        kind = last if level_num == TURNED else level_num
+        span = spans[kind]
+        first = capacity * sum(spans[:kind])
         size = capacity * span
+        to = rows * first + r * size
+        if kind == last:
+            place = 1 if level_num == TURNED else 0
+            first, to, size = first + place * span, to + place * span, half
         return pltpu.make_async_remote_copy(
             stage.at[block, dr - 1, pl.ds(first, size)],
-            fetched.at[block, pl.ds(pl.multiple_of(off + r * size, size), size)],
+            fetched.at[block, pl.ds(pl.multiple_of(to, half), size)],
             row_send.at[block, dr, level_num], row_recv.at[block, dr, level_num],
             device_id={"row": lax.rem(r - dr + rows, rows)}, device_id_type=MESH,
         )
 
-    def pick(block):
-        for turn in range(rows):
-            dr = (turn + 1) % rows
+    across = sorted(range(1, rows), key=lambda dr: dr != rows // 2) + [0]
+
+    def pick(block, first_use=False):
+        for dr in across:
+            if first_use and dr != 0:
+                id_copy(dr).wait()
             off = 0
             for level_num in range(LEVELS):
                 span = spans[level_num]
@@ -764,26 +775,30 @@
                 if level_num == TURNED:
                     off += span
                     continue
+                held_rows = half if level_num == last else span
+                pack = min(PACK, held_rows)
                 for place in range(capacity):
                     asked = jnp.broadcast_to(
-                        ids_v[dr, level_num, pl.ds(block * capacity + place, 1), :], (PACK, lanes_wide)
+                        ids_v[dr, level_num, pl.ds(block * capacity + place, 1), :], (pack, lanes_wide)
                     )
                     total = None
                     for tile in range(local_tiles):
                         mask = jnp.where(asked == tile, 1.0, 0.0).astype(jnp.bfloat16)
-                        first = starts[level_num] + tile * span
-                        part = blocks_v[block, first:first + span, :].reshape(
-                            span // PACK, PACK, lanes_wide) * mask[None]
+                        first = starts[level_num] + tile * held_rows
+                        part = blocks_v[block, first:first + held_rows, :].reshape(
+                            held_rows // pack, pack, lanes_wide) * mask[None]
                         total = part if total is None else total + part
-                    total = total.reshape(span, lanes_wide)
+                    total = total.reshape(held_rows, lanes_wide)
                     if dr == 0:
                         at = pl.multiple_of(rows * capacity * off + r * size + place * span, span)
-                        fetched[block, pl.ds(at, span), :] = total
+                        fetched[block, pl.ds(at, held_rows), :] = total
                     else:
                         at = capacity * off + place * span
-                        stage[block, dr - 1, at:at + span, :] = total
+                        stage[block, dr - 1, at:at + held_rows, :] = total
                 if dr != 0:
                     row_copy(block, dr, level_num).start()
+                    if level_num == last:
+                        row_copy(block, dr, TURNED).start()
                 off += span
 
     turned_span = spans[TURNED]
@@ -821,8 +836,7 @@
     def settle(block):
         for dr in range(1, rows):
             for level_num in range(LEVELS):
-                if level_num != TURNED:
-                    row_copy(block, dr, level_num).wait_recv()
+                row_copy(block, dr, level_num).wait_recv()
 
     def weigh(first, last):
         def one(step, carry):
@@ -857,7 +871,7 @@
 
     order = group_order(c, cols)
     mixed[...] = jnp.zeros_like(mixed)
-    pick(order[0])
+    pick(order[0], True)
     total_steps = local_tiles * head_count
     index_copy.wait()
 
@@ -887,7 +901,31 @@
     for g in range(1, cols):
         turned_copy(order[g], order[g]).wait_recv()
     mix([(order[g], TURNED) for g in range(1, cols)])
+
+    def row_sent(block):
+        for dr in range(1, rows):
+            for level_num in range(LEVELS):
+                row_copy(block, dr, level_num).wait_send()
+
+    for dr in range(1, rows):
+        layer_copy(dr).wait_send()
+    for dc in range(1, cols):
+        list_copy(dc).wait_send()
+        turned_copy(c, lax.rem(c + dc, cols)).wait_send()
+    for g in range(cols - 1):
+        row_sent(order[g])
+    for block in range(cols):
+        for part in range(parts):
+            @pl.when((block <= c) & (c < cols - 1))
+            def _(block=block, part=part):
+                up(block, part).wait_send()
+
+            @pl.when((block >= c) & (c > 0))
+            def _(block=block, part=part):
+                down(block, part).wait_send()
+
     mix_straight(order[cols - 1], send_sum)
+    row_sent(order[cols - 1])
 
     size = mixed.shape[2]
     ch = head_count * head_dim
@@ -919,33 +957,15 @@
         mine = mine - mean
         rest = rest - mean
         variance = jnp.sum(mine * mine + rest * rest, axis=1, keepdims=True) * scale
-        out_ref[pl.ds(pl.multiple_of(b * size, size), size), :] = mine * lax.rsqrt(variance + 1e-05)
+        normed = mine * lax.rsqrt(variance + 1e-05) * gain_ref[...] + shift_ref[...]
+        out_ref[pl.ds(pl.multiple_of(b * size, size), size), :] = normed.astype(jnp.bfloat16)
         return carry
 
     lax.fori_loop(0, local_tiles, finish_block, 0)
 
-    for dr in range(1, rows):
-        layer_copy(dr).wait_send()
-        for block in range(cols):
-            for level_num in range(LEVELS):
-                if level_num != TURNED:
-                    row_copy(block, dr, level_num).wait_send()
-    for dc in range(1, cols):
-        list_copy(dc).wait_send()
-        turned_copy(c, lax.rem(c + dc, cols)).wait_send()
-    for block in range(cols):
-        for part in range(parts):
-            @pl.when((block <= c) & (c < cols - 1))
-            def _(block=block, part=part):
-                up(block, part).wait_send()
-
-            @pl.when((block >= c) & (c > 0))
-            def _(block=block, part=part):
-                down(block, part).wait_send()
-
 
 def fused_layer(queries, level_blocks, tile_lists, samples, logit_weight, logit_bias, output_weight,
-                output_bias, sides, spans):
+                output_bias, norm_gain, norm_shift, sides, spans):
     rows = lax.axis_size("row")
     cols = lax.axis_size("col")
     tile_rows, tile_cols, level_count, per_block = tile_lists.shape
@@ -964,14 +984,15 @@
         tile_lists.reshape(local_tiles, level_count, per_block), level_blocks[3],
         queries.reshape(local_tiles, pixels, queries.shape[2]), logit_weight.T, logit_bias[None, :],
         samples.reshape(local_tiles, pixels, lanes), output_weight, output_bias[None, :],
+        norm_gain[None, :], norm_shift[None, :],
     )
     vmem = pl.BlockSpec(memory_space=pltpu.VMEM)
     dma = pltpu.SemaphoreType.DMA
-    parts = 3
+    parts = 2
     return pl.pallas_call(
         functools.partial(fused_kernel, sides, spans, per_block, head_count, head_dim, rows, cols),
-        out_shape=jax.ShapeDtypeStruct((local_tiles * pixels, channels), jnp.float32),
-        in_specs=[pl.BlockSpec(memory_space=pltpu.HBM)] * 11,
+        out_shape=jax.ShapeDtypeStruct((local_tiles * pixels, channels), jnp.bfloat16),
+        in_specs=[pl.BlockSpec(memory_space=pltpu.HBM)] * 13,
         out_specs=vmem,
         scratch_shapes=[
             *[pltpu.VMEM(one.shape, one.dtype) for one in held],
@@ -979,7 +1000,7 @@
             pltpu.VMEM((cols, requests // cols, channels), jnp.int32),
             pltpu.VMEM((cols, requests // cols, channels), jnp.int32),
             pltpu.VMEM((cols, rows * capacity * spans[TURNED], channels), jnp.bfloat16),
-            pltpu.VMEM((cols, local_tiles * (tile_span - spans[TURNED]), channels), jnp.bfloat16),
+            pltpu.VMEM((cols, local_tiles * (tile_span - spans[TURNED] - PACK // 2), channels), jnp.bfloat16),
             pltpu.VMEM((rows, LEVELS, requests // rows, channels), jnp.int32),
             pltpu.VMEM((rows, LEVELS, requests // rows, channels), jnp.int32),
             pltpu.VMEM((cols, rows - 1, capacity * tile_span, channels), jnp.bfloat16),
@@ -1001,7 +1022,7 @@
             dma((cols, parts)), dma((cols, parts)), dma((cols, parts)), dma((cols, parts)),
             dma((cols, rows, LEVELS)), dma((cols, rows, LEVELS)),
             dma((head_count,)), dma((head_count,)), dma((rows,)), dma((rows,)),
-            dma((cols,)), dma((cols,)), dma((cols,)), dma((cols,)), dma, dma((11,)),
+            dma((cols,)), dma((cols,)), dma((cols,)), dma((cols,)), dma, dma((13,)),
         ],
         compiler_params=pltpu.CompilerParams(
             collective_id=1, has_side_effects=True, vmem_limit_bytes=44 * 1024 * 1024
@@ -1042,9 +1063,8 @@
     if full:
         updated = fused_layer(
             queries, level_blocks, tile_lists, samples, logit_weight, logit_bias, output_weight,
-            output_bias, sides, spans
-        )
-        updated = (updated * norm_gain + norm_shift).astype(jnp.bfloat16)
+            output_bias, norm_gain, norm_shift, sides, spans
+        )
         return updated.reshape(tile_rows * tile_side, tile_cols * tile_side, channels)
     attn_out = gathered_attention(
         queries, level_blocks, tile_lists, samples, logit_weight, logit_bias, sides, spans

time: 44.1 us -> 43.1 us (0.977)
  Pallas kernels: 43.1 us -> 42.2 us
  other arithmetic: 0.76 us -> 0 us
  local copies, waits for them, and re-layouts: 0.01 us -> 0.71 us
    pallas_call x1, Pallas kernels: 43.1 us -> 42.2 us  [fused_layer(): pl.pallas_call(functools.partial(fused_kernel, sides, spans, per_block, h...]
    convert_element_type x1 -> x0, other arithmetic: 0.76 us -> none  [on_device(): updated = (updated * norm_gain + norm_shift).astype(jnp.bfloat16)]
    unnamed x4 -> x1, local copies, waits for them, and re-layouts: 0.01 us -> 0.71 us
where the time goes in v4:
time: 43.1 us; the launch traced here: 42.9 us
  Pallas kernels  42.2 us (98%)
  local copies, waits for them, and re-layouts  0.71 us (2%)
    pallas_call x1, Pallas kernels, fused_layer(): pl.pallas_call(functools.partial(fused_kernel, sides, spans, per_block, h...  42.2 us

profile of v4, /device:TPU:0, one launch (start us, length us, event | category | flops | bytes accessed | tf_op | source)
XLA Modules:
  0.0 42.9 jit_solution(11845310401164554191)
XLA Ops:
  0.0 42.2 %fused.1 = bf16[1024,128]{1,0:T(8,128)(2,1)S(1)} custom-call(bf16[1024,128]{1,0:T(8,128)(2,1)} %bitcast.15, bf16[256,128]{1,0:T(8,128)(2,1)} %bitcast.16, bf16[64,128]{1,0:T(8,128)(2,1)} %bitcast.18, s32[4,4,8]{2,1,0:T(4,128)} %bitcast.19, bf16[8,2,128]{2,1,0:T(2,128)(2,1)} %refs_4_.1, bf16[4,256,256]{2,1,0:T(8,128)(2,1)} %bitcast.13, ...), custom_call_target="tpu_custom_call" | custom-call | tf_op jit(solution)/shard_map/fused/pallas_call | solution.py:992
  42.2 0.7 %copy.15 = bf16[64,16,128]{2,1,0:T(8,128)(2,1)} copy(bf16[64,16,128]{2,1,0:T(8,128)(2,1)S(1)} %bitcast.12) | data formatting | bytes 524288
